TPU v7x, 32 devices: a 4x4x1 block of a 4x4x8 slice. The times are simulated.
32 devices in a mesh: data: 1 (over z), col: 4 (over y), row: 8 (over x, core).
Axes of the slice: x: 4, y: 4, z: 1, core: 2. Of those that a mesh axis runs over, the one named last changes fastest.
The devices are a block of a 4x4x8 slice.
Arguments:
- x_seq: bfloat16 [24, 16, 5760], P(None, 'data', 'row')
- h_init: float32 [2, 16, 5760], P(None, 'data', 'row')
- wx_l1: bfloat16 [5760, 3, 5760], P('row', None, 'col')
- whru_l1: bfloat16 [5760, 2, 5760], P('row', None, 'col')
- whn_l1: bfloat16 [5760, 5760], P('row', 'col')
- bias_l1: float32 [3, 5760], P(None, 'col')
- wx_l2: bfloat16 [5760, 3, 5760], P('row', None, 'col')
- whru_l2: bfloat16 [5760, 2, 5760], P('row', None, 'col')
- whn_l2: bfloat16 [5760, 5760], P('row', 'col')
- bias_l2: float32 [3, 5760], P(None, 'col')
Outputs:
- output 1: bfloat16 [24, 16, 5760], P(None, 'data', ('col', 'row'))
- output 2: float32 [2, 16, 5760], P(None, 'data', ('col', 'row'))
All inputs are finite; a program needn't handle non-finite values.
Results may differ from a plain program's by a relative error of at most 0.00249154.
Values are sent between devices in bfloat16 or wider.
A program may use at most 768 MiB of HBM per device.

v0:
```python
import jax
import jax.numpy as jnp
from jax import lax
from jax.sharding import PartitionSpec as P


def solution(mesh):
    row_count = mesh.shape["row"]
    seq_spec = P(None, "data", "row")
    out_spec = P(None, "data", ("col", "row"))
    wide_spec = P("row", None, "col")
    square_spec = P("row", "col")
    bias_spec = P(None, "col")

    def gather_rows(col_part, row_idx, row_block):
        gathered = lax.all_gather(col_part, "col", axis=1, tiled=True)
        return lax.dynamic_slice_in_dim(gathered, row_idx * row_block, row_block, axis=1)

    def own_part(col_part, row_idx):
        unit_block = col_part.shape[-1] // row_count
        return lax.dynamic_slice_in_dim(col_part, row_idx * unit_block, unit_block, axis=col_part.ndim - 1)

    def gru_layer(in_rows, h_col, h_row, w_x, w_hru, w_hn, gate_bias, keep_rows):
        row_idx = lax.axis_index("row")
        row_block = in_rows.shape[2]

        def gru_step(state_pair, step_in):
            h_prev, prev_row = state_pair
            in_part = jnp.einsum("bk,kgn->bgn", step_in, w_x, preferred_element_type=jnp.float32)
            rec_part = jnp.einsum("bk,kgn->bgn", prev_row, w_hru, preferred_element_type=jnp.float32)
            part_sum = jnp.concatenate([in_part[:, :2] + rec_part, in_part[:, 2:]], axis=1)
            gate_pre = lax.psum(part_sum, "row") + gate_bias
            reset_gate = jax.nn.sigmoid(gate_pre[:, 0])
            update_gate = jax.nn.sigmoid(gate_pre[:, 1])
            gated_row = gather_rows((reset_gate * h_prev).astype(jnp.bfloat16), row_idx, row_block)
            cand_pre = lax.psum(jnp.dot(gated_row, w_hn, preferred_element_type=jnp.float32), "row")
            candidate = jnp.tanh(gate_pre[:, 2] + cand_pre)
            h_next = (1.0 - update_gate) * candidate + update_gate * h_prev
            next_row = gather_rows(h_next.astype(jnp.bfloat16), row_idx, row_block)
            if keep_rows:
                step_out = next_row
            else:
                step_out = own_part(h_next, row_idx).astype(jnp.bfloat16)
            return (h_next, next_row), step_out

        final_pair, seq_out = lax.scan(gru_step, (h_col, h_row), in_rows)
        return final_pair[0], seq_out

    def device_body(x_rows, h_rows, wx_l1, whru_l1, whn_l1, bias_l1, wx_l2, whru_l2, whn_l2, bias_l2):
        row_idx = lax.axis_index("row")
        col_idx = lax.axis_index("col")
        col_block = wx_l1.shape[2]
        h_gathered = lax.all_gather(h_rows, "row", axis=2, tiled=True)
        h_cols = lax.dynamic_slice_in_dim(h_gathered, col_idx * col_block, col_block, axis=2)
        h_starts = h_rows.astype(jnp.bfloat16)
        h1_last, h1_rows = gru_layer(x_rows, h_cols[0], h_starts[0], wx_l1, whru_l1, whn_l1, bias_l1, True)
        h2_last, h2_own = gru_layer(h1_rows, h_cols[1], h_starts[1], wx_l2, whru_l2, whn_l2, bias_l2, False)
        h_final = jnp.stack([own_part(h1_last, row_idx), own_part(h2_last, row_idx)])
        return h2_own, h_final

    return jax.shard_map(
        device_body,
        mesh=mesh,
        in_specs=(seq_spec, seq_spec, wide_spec, wide_spec, square_spec, bias_spec, wide_spec, wide_spec, square_spec, bias_spec),
        out_specs=(out_spec, out_spec),
        check_vma=False,
    )
```

profile of v0, /device:TPU:97, one launch (start us, length us, event | category | flops | bytes accessed | tf_op | source)
XLA Modules:
  0.0 6843.4 jit_solution(2843050575455430192)
XLA Ops:
  58.0 3386.7 %while.32 = (s32[]{:T(128)}, f32[16,1440]{1,0:T(8,128)S(1)}, bf16[16,720]{1,0:T(8,128)(2,1)S(1)}, bf16[24,16,720]{2,1,0:T(8,128)(2,1)}, bf16[24,16,720]{2,1,0:T(...) while((s32[]{:T(128)}, f32[16,1440]{1,0:T(8,128)S(1)}, ...), condition=%wide.region_3.4_spmd, body=%wide.region_0.3_spmd.sunk | while | flops 199664640 | bytes 36728432 | solution.py:46
  63.8 56.5 all-reduce.5.cloned.1.call-done
  273.6 55.7 all-reduce.7.cloned.1.call-done
  414.7 55.7 all-reduce.7.cloned.1.call-done
  555.8 55.7 all-reduce.7.cloned.1.call-done
  696.8 55.7 all-reduce.7.cloned.1.call-done
  837.9 55.7 all-reduce.7.cloned.1.call-done
  978.9 55.7 all-reduce.7.cloned.1.call-done
  1261.0 55.7 all-reduce.7.cloned.1.call-done
  1402.1 55.7 all-reduce.7.cloned.1.call-done
  1543.2 55.7 all-reduce.7.cloned.1.call-done
  1684.2 55.7 all-reduce.7.cloned.1.call-done
  1825.3 55.7 all-reduce.7.cloned.1.call-done
  2107.4 55.7 all-reduce.7.cloned.1.call-done
  2248.4 55.7 all-reduce.7.cloned.1.call-done
  2530.5 55.7 all-reduce.7.cloned.1.call-done
  2671.6 55.7 all-reduce.7.cloned.1.call-done
  2812.7 55.7 all-reduce.7.cloned.1.call-done
  2953.7 55.7 all-reduce.7.cloned.1.call-done
  3094.8 55.7 all-reduce.7.cloned.1.call-done
  3235.8 55.7 all-reduce.7.cloned.1.call-done
  3376.9 55.7 all-reduce.7.cloned.1.call-done
  3451.2 3385.0 %while.33 = (s32[]{:T(128)}, f32[16,1440]{1,0:T(8,128)S(1)}, bf16[16,720]{1,0:T(8,128)(2,1)S(1)}, bf16[24,16,180]{2,1,0:T(8,128)(2,1)}, bf16[24,16,720]{2,1,0:T(...) while((s32[]{:T(128)}, f32[16,1440]{1,0:T(8,128)S(1)}, ...), condition=%wide.region_7.8_spmd, body=%wide.region_4.7_spmd.sunk | while | flops 199664640 | bytes 36694776 | solution.py:46
  3524.4 55.7 all-reduce.11.cloned.1.call-done
  (1153 shorter events, 5599.5 us)
Async XLA Ops:
  63.7 124.6 %all-reduce.7.cloned.1.call-start = ((), (), s32[]{:S(2)}) async-start(), calls=%async_computation.1 | async-start | bytes 196608 | tf_op jit(solution)/shard_map/while/body/eval_jaxpr/psum | solution.py:36
  206.1 123.3 %all-reduce.7.cloned.1.call-start = ((), (), s32[]{:S(2)}) async-start(), calls=%async_computation.1 | async-start | bytes 196608 | tf_op jit(solution)/shard_map/while/body/eval_jaxpr/psum | solution.py:36
  347.1 123.3 %all-reduce.7.cloned.1.call-start = ((), (), s32[]{:S(2)}) async-start(), calls=%async_computation.1 | async-start | bytes 196608 | tf_op jit(solution)/shard_map/while/body/eval_jaxpr/psum | solution.py:36
  488.2 123.3 %all-reduce.7.cloned.1.call-start = ((), (), s32[]{:S(2)}) async-start(), calls=%async_computation.1 | async-start | bytes 196608 | tf_op jit(solution)/shard_map/while/body/eval_jaxpr/psum | solution.py:36
  629.3 123.3 %all-reduce.7.cloned.1.call-start = ((), (), s32[]{:S(2)}) async-start(), calls=%async_computation.1 | async-start | bytes 196608 | tf_op jit(solution)/shard_map/while/body/eval_jaxpr/psum | solution.py:36
  770.3 123.3 %all-reduce.7.cloned.1.call-start = ((), (), s32[]{:S(2)}) async-start(), calls=%async_computation.1 | async-start | bytes 196608 | tf_op jit(solution)/shard_map/while/body/eval_jaxpr/psum | solution.py:36
  911.4 123.3 %all-reduce.7.cloned.1.call-start = ((), (), s32[]{:S(2)}) async-start(), calls=%async_computation.1 | async-start | bytes 196608 | tf_op jit(solution)/shard_map/while/body/eval_jaxpr/psum | solution.py:36
  1052.4 123.3 %all-reduce.7.cloned.1.call-start = ((), (), s32[]{:S(2)}) async-start(), calls=%async_computation.1 | async-start | bytes 196608 | tf_op jit(solution)/shard_map/while/body/eval_jaxpr/psum | solution.py:36
  1193.5 123.3 %all-reduce.7.cloned.1.call-start = ((), (), s32[]{:S(2)}) async-start(), calls=%async_computation.1 | async-start | bytes 196608 | tf_op jit(solution)/shard_map/while/body/eval_jaxpr/psum | solution.py:36
  1334.5 123.3 %all-reduce.7.cloned.1.call-start = ((), (), s32[]{:S(2)}) async-start(), calls=%async_computation.1 | async-start | bytes 196608 | tf_op jit(solution)/shard_map/while/body/eval_jaxpr/psum | solution.py:36
  1475.6 123.3 %all-reduce.7.cloned.1.call-start = ((), (), s32[]{:S(2)}) async-start(), calls=%async_computation.1 | async-start | bytes 196608 | tf_op jit(solution)/shard_map/while/body/eval_jaxpr/psum | solution.py:36
  1616.7 123.3 %all-reduce.7.cloned.1.call-start = ((), (), s32[]{:S(2)}) async-start(), calls=%async_computation.1 | async-start | bytes 196608 | tf_op jit(solution)/shard_map/while/body/eval_jaxpr/psum | solution.py:36
  1757.7 123.3 %all-reduce.7.cloned.1.call-start = ((), (), s32[]{:S(2)}) async-start(), calls=%async_computation.1 | async-start | bytes 196608 | tf_op jit(solution)/shard_map/while/body/eval_jaxpr/psum | solution.py:36
  1898.8 123.3 %all-reduce.7.cloned.1.call-start = ((), (), s32[]{:S(2)}) async-start(), calls=%async_computation.1 | async-start | bytes 196608 | tf_op jit(solution)/shard_map/while/body/eval_jaxpr/psum | solution.py:36
  2039.8 123.3 %all-reduce.7.cloned.1.call-start = ((), (), s32[]{:S(2)}) async-start(), calls=%async_computation.1 | async-start | bytes 196608 | tf_op jit(solution)/shard_map/while/body/eval_jaxpr/psum | solution.py:36
  2180.9 123.3 %all-reduce.7.cloned.1.call-start = ((), (), s32[]{:S(2)}) async-start(), calls=%async_computation.1 | async-start | bytes 196608 | tf_op jit(solution)/shard_map/while/body/eval_jaxpr/psum | solution.py:36
  2321.9 123.3 %all-reduce.7.cloned.1.call-start = ((), (), s32[]{:S(2)}) async-start(), calls=%async_computation.1 | async-start | bytes 196608 | tf_op jit(solution)/shard_map/while/body/eval_jaxpr/psum | solution.py:36
  2463.0 123.3 %all-reduce.7.cloned.1.call-start = ((), (), s32[]{:S(2)}) async-start(), calls=%async_computation.1 | async-start | bytes 196608 | tf_op jit(solution)/shard_map/while/body/eval_jaxpr/psum | solution.py:36
  2604.0 123.3 %all-reduce.7.cloned.1.call-start = ((), (), s32[]{:S(2)}) async-start(), calls=%async_computation.1 | async-start | bytes 196608 | tf_op jit(solution)/shard_map/while/body/eval_jaxpr/psum | solution.py:36
  2745.1 123.3 %all-reduce.7.cloned.1.call-start = ((), (), s32[]{:S(2)}) async-start(), calls=%async_computation.1 | async-start | bytes 196608 | tf_op jit(solution)/shard_map/while/body/eval_jaxpr/psum | solution.py:36
  2886.1 123.3 %all-reduce.7.cloned.1.call-start = ((), (), s32[]{:S(2)}) async-start(), calls=%async_computation.1 | async-start | bytes 196608 | tf_op jit(solution)/shard_map/while/body/eval_jaxpr/psum | solution.py:36
  3027.2 123.3 %all-reduce.7.cloned.1.call-start = ((), (), s32[]{:S(2)}) async-start(), calls=%async_computation.1 | async-start | bytes 196608 | tf_op jit(solution)/shard_map/while/body/eval_jaxpr/psum | solution.py:36
  3168.3 123.3 %all-reduce.7.cloned.1.call-start = ((), (), s32[]{:S(2)}) async-start(), calls=%async_computation.1 | async-start | bytes 196608 | tf_op jit(solution)/shard_map/while/body/eval_jaxpr/psum | solution.py:36
  3309.3 123.3 %all-reduce.7.cloned.1.call-start = ((), (), s32[]{:S(2)}) async-start(), calls=%async_computation.1 | async-start | bytes 196608 | tf_op jit(solution)/shard_map/while/body/eval_jaxpr/psum | solution.py:36
  (125 other events, 6149.4 us)
Sparse Core Ops, SparseCore 0:
  63.9 56.3 all-reduce.4
  273.8 55.5 all-reduce.6
  414.8 55.5 all-reduce.6
  555.9 55.5 all-reduce.6
  696.9 55.5 all-reduce.6
  838.0 55.5 all-reduce.6
  979.0 55.5 all-reduce.6
  1120.1 55.5 all-reduce.6
  1261.2 55.5 all-reduce.6
  1402.2 55.5 all-reduce.6
  1543.3 55.5 all-reduce.6
  1684.3 55.5 all-reduce.6
  1825.4 55.5 all-reduce.6
  1966.4 55.5 all-reduce.6
  2107.5 55.5 all-reduce.6
  2248.6 55.5 all-reduce.6
  2389.6 55.5 all-reduce.6
  2530.7 55.5 all-reduce.6
  2671.7 55.5 all-reduce.6
  2812.8 55.5 all-reduce.6
  2953.8 55.5 all-reduce.6
  3094.9 55.5 all-reduce.6
  3235.9 55.5 all-reduce.6
  3377.0 55.5 all-reduce.6
  (72 shorter events, 3974.6 us)
where the time goes:
time: 6850 us; the launch traced here: 6840 us
  waiting for transfers between devices  5330 us (78%)
  blocking collectives  988 us (14%)
  matrix products  277 us (4%)
  other arithmetic  133 us (2%)
  local copies, waits for them, and re-layouts  94.5 us (1%)
    psum x48, waiting for transfers between devices, gru_step(): lax.psum(jnp.dot(gated_row, w_hn, preferred_element_type=jnp.float32), 'r...  2670 us
    psum x48, waiting for transfers between devices, gru_step(): gate_pre = lax.psum(part_sum, 'row') + gate_bias  2650 us
    all_gather x96, blocking collectives, gather_rows(): gathered = lax.all_gather(col_part, 'col', axis=1, tiled=True)  945 us
    dot_general x48, matrix products, gru_step(): jnp.einsum('bk,kgn->bgn', step_in, w_x, preferred_element_type=jnp.float32)  192 us
  transfers between devices with their start and end apart: 96, of which 96 were waited for; matrix products, arithmetic and copies ran while one was open for 0% of the time, Pallas kernels for 0%

commit v1 on v0

v1 whole, which is shorter than its diff:
```python
import functools

import jax
import jax.numpy as jnp
from jax import lax
from jax.experimental import pallas as pl
from jax.experimental.pallas import tpu as pltpu
from jax.sharding import PartitionSpec as P

MESH = pl.DeviceIdType.MESH
F32 = jnp.float32
BF16 = jnp.bfloat16
LANES = 128

H1, RH1, H2, RH2 = range(4)
R1, N1, R2, N2 = range(4)
XR, XU, XN, PR, PU, PN, U1, U2 = range(8)
RING = 4


def cdiv(a, b):
    return -(-a // b)


def gru_kernel(dims, *refs):
    steps, batch, rows, cols, nx, ny, chunk = dims
    (x_hbm, h0, wx1, wru1u, wru1r, wn1, b1, wx2, wru2u, wru2r, wn2, b2,
     seq_out, fin_out,
     w_own, w_blk, xb, hcat, h0s, state, ag_src, ag_buf, hs, bias, bpad,
     p_u1, p_x, p_p, p_u2, s_u1, s_x, s_p, s_u2, xu_keep, pu_keep,
     blk, out_n, out_s, fin_src, fin_buf, fblk, fin_n, fin_s,
     ld_sem, wl_sem, wsend, wrecv, bs_send, bs_recv, x_sem, i_sem,
     ag_send, ag_recv, hs_send, hs_recv, rs_send, rs_recv, f_sem, o_sem) = refs
    block = 2 * rows
    device_row = lax.axis_index("row")
    y = lax.axis_index("col")
    x = device_row // 2
    core = lax.rem(device_row, 2)

    def wrap(v, n):
        return lax.rem(v + n, n)

    def remote(src, dst, ssem, rsem, tx, tc, ty):
        return pltpu.make_async_remote_copy(
            src_ref=src, dst_ref=dst, send_sem=ssem, recv_sem=rsem,
            device_id={"row": tx * 2 + tc, "col": ty}, device_id_type=MESH,
        )

    def wait_in(dst, sem):
        pltpu.make_async_copy(dst, dst, sem).wait()

    def hop(d, n):
        return min(d, n - d)

    offsets = [(dx, dy) for dx in range(nx) for dy in range(ny) if (dx, dy) != (0, 0)]
    offsets.sort(key=lambda o: hop(o[0], nx) + hop(o[1], ny))
    dists = [hop(dx, nx) + hop(dy, ny) for dx, dy in offsets]
    groups = []
    for d in sorted(set(dists)):
        first = dists.index(d)
        groups.append((first, first + dists.count(d)))
    peers = len(offsets)

    barrier = pltpu.get_barrier_semaphore()
    for d in range(1, 2 * nx * ny):
        tr = lax.rem(device_row + d % (2 * nx), 2 * nx)
        ty = lax.rem(y + d // (2 * nx), ny)
        pl.semaphore_signal(barrier, inc=1, device_id={"row": tr, "col": ty}, device_id_type=MESH)

    moved = ((wru1r, R1), (wn1, N1), (wru2r, R2), (wn2, N2))
    kept = ((wx1.at[0], XR), (wx1.at[1], XU), (wx1.at[2], XN), (wru1u, U1),
            (wx2.at[0], PR), (wx2.at[1], PU), (wx2.at[2], PN), (wru2u, U2))

    my_rows = pl.ds(pl.multiple_of(device_row * rows, 16), rows)

    def column_slice(i):
        return pl.ds(pl.multiple_of(i * chunk, LANES), chunk)

    @pl.when(core == 0)
    def _():
        loads = []
        for src, u in kept:
            loads.append(pltpu.make_async_copy(src, w_blk.at[u, pl.ds(0, rows)], ld_sem.at[u]))
        xload = pltpu.make_async_copy(x_hbm, xb.at[0], x_sem.at[0])
        xload.start()
        for c in loads:
            c.start()
        pl.semaphore_wait(barrier, 2 * nx * ny - 1)
        for src, u in moved:
            for d in range(nx):
                tx = wrap(x + d, nx)
                remote(src.at[:, column_slice(tx)], w_own.at[u, my_rows], wsend.at[u], wrecv.at[u], tx, 1, y).start()

        @pl.when(x == y)
        def _():
            remote(h0, h0s, i_sem.at[0], i_sem.at[1], x, 1, y).start()

        xload.wait()
        wait_in(xb.at[1], x_sem.at[1])
        for u in range(8):
            loads[u].wait()
            wait_in(w_blk.at[kept[u][1], pl.ds(rows, rows)], bs_recv.at[kept[u][1]])

        def row_dot(vec, u):
            return jnp.dot(vec, w_blk[u], preferred_element_type=F32)

        def spread(src, dst, kind, slot):
            for d in range(nx):
                tx = wrap(x + d, nx)
                remote(src.at[:, :, column_slice(tx)], dst.at[slot, x], rs_send.at[kind], rs_recv.at[kind, slot], tx, 1, y).start()

        def spread_wait(src, kind):
            wait_in(src, rs_send.at[kind])

        def project(t):
            def half(g):
                return (jnp.dot(xb[0, t], w_blk[g, 0:rows], preferred_element_type=F32)
                        + jnp.dot(xb[1, t], w_blk[g, rows:block], preferred_element_type=F32))
            s_x[0, :, 0:block] = half(XR)
            s_x[1, :, 0:block] = half(XN)
            spread(s_x, p_x, 1, lax.rem(t, RING))
            xu_keep[...] = half(XU)

        s_u1[...] = jnp.zeros_like(s_u1)
        s_u2[...] = jnp.zeros_like(s_u2)
        s_x[...] = jnp.zeros_like(s_x)
        s_p[...] = jnp.zeros_like(s_p)
        project(0)

        def step(i, carry):
            wait_in(hs.at[0, 0], hs_recv.at[0, lax.rem(i, 2)])
            h1v = hs[0, lax.rem(i, 2), :, 0:block]

            @pl.when(i < steps)
            def _():
                @pl.when(i > 0)
                def _():
                    spread_wait(s_u1, 0)
                s_u1[0, :, 0:block] = row_dot(h1v, U1) + xu_keep[...]
                spread(s_u1, p_u1, 0, lax.rem(i, RING))

            @pl.when(i >= 1)
            def _():
                @pl.when(i > 1)
                def _():
                    spread_wait(s_p, 2)
                s_p[0, :, 0:block] = row_dot(h1v, PR)
                s_p[1, :, 0:block] = row_dot(h1v, PN)
                spread(s_p, p_p, 2, lax.rem(i - 1, RING))
                pu_keep[...] = row_dot(h1v, PU)
                wait_in(hs.at[1, 0], hs_recv.at[1, lax.rem(i, 2)])

                @pl.when(i > 1)
                def _():
                    spread_wait(s_u2, 3)
                s_u2[0, :, 0:block] = row_dot(hs[1, lax.rem(i, 2), :, 0:block], U2) + pu_keep[...]
                spread(s_u2, p_u2, 3, lax.rem(i - 1, RING))

            @pl.when(i + 1 < steps)
            def _():
                spread_wait(s_x, 1)
                project(i + 1)
            return carry

        lax.fori_loop(0, steps + 1, step, 0)
        spread_wait(s_u1, 0)
        spread_wait(s_x, 1)
        spread_wait(s_p, 2)
        spread_wait(s_u2, 3)
        for u in range(4):
            wait_in(w_own.at[0, pl.ds(0, nx * rows)], wsend.at[u])

        @pl.when(x == y)
        def _():
            wait_in(h0, i_sem.at[0])
        wait_in(out_s, o_sem.at[1])
        wait_in(fin_s, o_sem.at[3])
        seq_out[...] = out_s[...]
        fin_out[...] = fin_s[...]

    @pl.when(core == 1)
    def _():
        own = []
        for src, u in moved:
            own.append(pltpu.make_async_copy(src.at[:, column_slice(x)], w_own.at[u, my_rows], wl_sem.at[u]))
        for c in own:
            c.start()
        pl.semaphore_wait(barrier, 2 * nx * ny - 1)
        remote(x_hbm, xb.at[1], x_sem.at[0], x_sem.at[1], x, 0, y).start()
        for src, u in kept[:4]:
            remote(src, w_blk.at[u, pl.ds(rows, rows)], bs_send.at[u], bs_recv.at[u], x, 0, y).start()
        for src, u in moved:
            for d in range(1, nx):
                tx = wrap(x + d, nx)
                remote(src.at[:, column_slice(tx)], w_own.at[u, my_rows], wsend.at[u], wrecv.at[u], tx, 1, y).start()
        for src, u in kept[4:]:
            remote(src, w_blk.at[u, pl.ds(rows, rows)], bs_send.at[u], bs_recv.at[u], x, 0, y).start()

        for u in range(4):
            w_own[u, pl.ds(nx * block, chunk * nx - block)] = jnp.zeros((chunk * nx - block, chunk), BF16)
        bpad[...] = jnp.zeros_like(bpad)
        bpad[0, 0:3, 0:block] = b1[...]
        bpad[1, 0:3, 0:block] = b2[...]
        bias[...] = bpad[:, :, column_slice(x)]
        valid = jnp.minimum(block - x * chunk, chunk)
        keep = lax.broadcasted_iota(jnp.int32, (batch, chunk), 1) < valid

        @pl.when(x == y)
        def _():
            wait_in(h0s, i_sem.at[1])
            hcat[...] = jnp.zeros_like(hcat)
            hcat[:, :, 0:rows] = h0s[...]
            hcat[:, :, rows:block] = h0[...]
            for d in range(1, nx):
                tx = wrap(x + d, nx)
                remote(hcat.at[:, :, column_slice(tx)], state, i_sem.at[2], i_sem.at[3], tx, 1, y).start()
            state[...] = hcat[:, :, column_slice(x)]
            wait_in(hcat.at[:, :, pl.ds(0, (nx - 1) * chunk)], i_sem.at[2])

        @pl.when(x != y)
        def _():
            wait_in(state, i_sem.at[3])

        def to_all(kind):
            for k in reversed(range(peers)):
                dx, dy = offsets[k]
                g = [j for j, (a, b) in enumerate(groups) if a <= k < b][0]
                remote(ag_src.at[kind], ag_buf.at[kind, k], ag_send.at[kind], ag_recv.at[kind, g],
                       wrap(x + dx, nx), 1, wrap(y + dy, ny)).start()

        def to_blocks(layer, slot):
            for d in range(ny):
                remote(ag_src.at[H1 if layer == 0 else H2], hs.at[layer, slot, :, column_slice(x)],
                       hs_send.at[layer], hs_recv.at[layer, slot], y, 0, wrap(y + d, ny)).start()

        def sent(kind):
            wait_in(ag_buf.at[kind], ag_send.at[kind])

        def sent_blocks(layer):
            wait_in(ag_buf.at[0, pl.ds(0, ny)], hs_send.at[layer])

        def weight_rows(dx, dy):
            sx, sy = wrap(x - dx, nx), wrap(y - dy, ny)
            return pl.ds(pl.multiple_of(sy * block + sx * chunk, 32), chunk)

        def gathered_dot(kind, u, acc):
            acc = acc + jnp.dot(ag_src[kind], w_own[u, weight_rows(0, 0)], preferred_element_type=F32)
            for g, (a, b) in enumerate(groups):
                wait_in(ag_buf.at[kind, pl.ds(a, b - a)], ag_recv.at[kind, g])
                for k in range(a, b):
                    acc = acc + jnp.dot(ag_buf[kind, k], w_own[u, weight_rows(*offsets[k])], preferred_element_type=F32)
            return acc

        def partial_sum(buf, slot, g):
            total = buf[slot, 0, g]
            for s in range(1, nx):
                total = total + buf[slot, s, g]
            return total

        def wait_weights(u):
            own[u].wait()
            wait_in(w_own.at[u, pl.ds(0, (2 * nx - 1) * rows)], wrecv.at[u])

        for layer in range(2):
            kind = H1 if layer == 0 else H2
            ag_src[kind] = jnp.where(keep, state[layer], 0.0).astype(BF16)
            to_all(kind)
            to_blocks(layer, layer)

        def copy_row_block():
            blk[:, column_slice(x)] = ag_src[H2]
            for k, (dx, dy) in enumerate(offsets):
                if dy == 0:
                    blk[:, column_slice(wrap(x - dx, nx))] = ag_buf[H2, k]

        def reset_phase(layer, kind, unit, slot, buf, sem):
            wait_in(buf.at[0], sem)
            pre = gathered_dot(kind, unit, partial_sum(buf, slot, 0) + bias[layer, 0:1])
            if layer == 1:
                copy_row_block()
            gate = jax.nn.sigmoid(pre)
            out = RH1 if layer == 0 else RH2
            ag_src[out] = jnp.where(keep, gate * state[layer], 0.0).astype(BF16)
            to_all(out)
            sent(kind)
            sent_blocks(layer)

        def candidate_phase(layer, unit, slot, buf, ubuf, usem):
            kind = RH1 if layer == 0 else RH2
            pre = gathered_dot(kind, unit, partial_sum(buf, slot, 1) + bias[layer, 2:3])
            cand = jnp.tanh(pre)
            wait_in(ubuf.at[0], usem)
            upd = jax.nn.sigmoid(partial_sum(ubuf, slot, 0) + bias[layer, 1:2])
            new = (1.0 - upd) * cand + upd * state[layer]
            state[layer] = new
            return jnp.where(keep, new, 0.0).astype(BF16)

        part = block // (2 * nx)

        def step(i, carry):
            @pl.when(i < steps)
            def _():
                @pl.when(i == 0)
                def _():
                    wait_weights(R1)
                slot = lax.rem(i, RING)
                reset_phase(0, H1, R1, slot, p_x, rs_recv.at[1, slot])

            @pl.when(i >= 2)
            def _():
                t = i - 2
                slot = lax.rem(t, RING)

                @pl.when(i == 2)
                def _():
                    wait_weights(N2)
                new = candidate_phase(1, N2, slot, p_p, p_u2, rs_recv.at[3, slot])
                sent(RH2)

                @pl.when(t < steps - 1)
                def _():
                    ag_src[H2] = new
                    to_all(H2)
                    to_blocks(1, lax.rem(t, 2))

            @pl.when(i < steps)
            def _():
                @pl.when(i == 0)
                def _():
                    wait_weights(N1)
                slot = lax.rem(i, RING)
                new = candidate_phase(0, N1, slot, p_x, p_u1, rs_recv.at[0, slot])
                sent(RH1)
                ag_src[H1] = new

                @pl.when(i < steps - 1)
                def _():
                    to_all(H1)
                to_blocks(0, lax.rem(i + 1, 2))

            @pl.when(jnp.logical_and(i >= 1, i < steps + 1))
            def _():
                @pl.when(i == 1)
                def _():
                    wait_weights(R2)
                slot = lax.rem(i - 1, RING)
                reset_phase(1, H2, R2, slot, p_p, rs_recv.at[2, slot])

                @pl.when(i >= 2)
                def _():
                    for k in range(nx):
                        @pl.when(x == k)
                        def _():
                            out_s[i - 2] = blk[:, 2 * k * part:(2 * k + 1) * part]
                            out_n[i - 2] = blk[:, (2 * k + 1) * part:(2 * k + 2) * part]
            return carry

        lax.fori_loop(0, steps + 2, step, 0)
        sent_blocks(0)

        fin_src[...] = state[...]
        for d in range(1, nx):
            tx = wrap(x + d, nx)
            remote(fin_src, fin_buf.at[d], f_sem.at[0], f_sem.at[1], tx, 1, y).start()
        fblk[:, :, column_slice(x)] = state[...]
        wait_in(fin_buf.at[pl.ds(1, nx - 1)], f_sem.at[1])
        for d in range(1, nx):
            fblk[:, :, column_slice(wrap(x - d, nx))] = fin_buf[d]
        for k in range(nx):
            @pl.when(x == k)
            def _():
                s_part = fblk[:, :, 2 * k * part:(2 * k + 1) * part]
                n_part = fblk[:, :, (2 * k + 1) * part:(2 * k + 2) * part]
                fin_s[...] = s_part
                fin_n[...] = n_part
                out_s[steps - 1] = s_part[1].astype(BF16)
                out_n[steps - 1] = n_part[1].astype(BF16)
        remote(fin_s, fin_s, o_sem.at[2], o_sem.at[3], x, 0, y).start()
        remote(out_s, out_s, o_sem.at[0], o_sem.at[1], x, 0, y).start()
        seq_out[...] = out_n[...]
        fin_out[...] = fin_n[...]
        wait_in(fin_s, o_sem.at[2])
        wait_in(out_s, o_sem.at[0])
        wait_in(fin_buf.at[pl.ds(1, nx - 1)], f_sem.at[0])
        wait_in(xb.at[1], x_sem.at[0])
        for u in range(4):
            wait_in(w_own.at[0, pl.ds(0, (nx - 1) * rows)], wsend.at[u])
        for u in range(8):
            wait_in(w_blk.at[0, pl.ds(rows, rows)], bs_send.at[u])


def solution(mesh):
    nx, ny = mesh.shape["row"] // 2, mesh.shape["col"]
    seq_spec = P(None, "data", "row")
    out_spec = P(None, "data", ("col", "row"))
    wide_spec = P("row", None, "col")
    square_spec = P("row", "col")
    bias_spec = P(None, "col")

    def device_body(x_rows, h_rows, wx_l1, whru_l1, whn_l1, bias_l1, wx_l2, whru_l2, whn_l2, bias_l2):
        steps, batch, rows = x_rows.shape
        cols = whn_l1.shape[1]
        chunk = cdiv(cdiv(cols, nx), LANES) * LANES
        wide = nx * chunk
        part = cols // (2 * nx)
        dims = (steps, batch, rows, cols, nx, ny, chunk)

        def padded(w):
            return jnp.pad(w, ((0, 0), (0, wide - cols)))

        peers = nx * ny - 1
        total_rows = nx * cols
        hbm = pl.BlockSpec(memory_space=pl.ANY)
        vmem = pl.BlockSpec(memory_space=pltpu.VMEM)
        dma = pltpu.SemaphoreType.DMA
        operands = []
        specs = []
        for lead, wx, wru, wn, b in (((x_rows, h_rows), wx_l1, whru_l1, whn_l1, bias_l1), ((), wx_l2, whru_l2, whn_l2, bias_l2)):
            if lead:
                operands += list(lead)
                specs += [hbm, vmem]
            operands += [jnp.transpose(wx, (1, 0, 2)), wru[:, 1], padded(wru[:, 0]), padded(wn), b]
            specs += [hbm, hbm, hbm, hbm, vmem]
        scratch = [
            pltpu.VMEM((4, total_rows + wide - cols, chunk), BF16),
            pltpu.VMEM((8, 2 * rows, cols), BF16),
            pltpu.VMEM((2, steps, batch, rows), BF16),
            pltpu.VMEM((2, batch, wide), F32),
            pltpu.VMEM((2, batch, rows), F32),
            pltpu.VMEM((2, batch, chunk), F32),
            pltpu.VMEM((4, batch, chunk), BF16),
            pltpu.VMEM((4, peers, batch, chunk), BF16),
            pltpu.VMEM((2, 2, batch, wide), BF16),
            pltpu.VMEM((2, 8, chunk), F32),
            pltpu.VMEM((2, 8, wide), F32),
            pltpu.VMEM((RING, nx, 1, batch, chunk), F32),
            pltpu.VMEM((RING, nx, 2, batch, chunk), F32),
            pltpu.VMEM((RING, nx, 2, batch, chunk), F32),
            pltpu.VMEM((RING, nx, 1, batch, chunk), F32),
            pltpu.VMEM((1, batch, wide), F32),
            pltpu.VMEM((2, batch, wide), F32),
            pltpu.VMEM((2, batch, wide), F32),
            pltpu.VMEM((1, batch, wide), F32),
            pltpu.VMEM((batch, cols), F32),
            pltpu.VMEM((batch, cols), F32),
            pltpu.VMEM((batch, wide), BF16),
            pltpu.VMEM((steps, batch, part), BF16),
            pltpu.VMEM((steps, batch, part), BF16),
            pltpu.VMEM((2, batch, chunk), F32),
            pltpu.VMEM((nx, 2, batch, chunk), F32),
            pltpu.VMEM((2, batch, wide), F32),
            pltpu.VMEM((2, batch, part), F32),
            pltpu.VMEM((2, batch, part), F32),
            dma((8,)),
            dma((4,)),
            dma((4,)),
            dma((4,)),
            dma((8,)),
            dma((8,)),
            dma((2,)),
            dma((4,)),
            dma((4,)),
            dma((4, 4)),
            dma((2,)),
            dma((2, 2)),
            dma((4,)),
            dma((4, RING)),
            dma((2,)),
            dma((4,)),
        ]
        return pl.pallas_call(
            functools.partial(gru_kernel, dims),
            name="gru",
            out_shape=(
                jax.ShapeDtypeStruct((steps, batch, part), BF16),
                jax.ShapeDtypeStruct((2, batch, part), F32),
            ),
            in_specs=specs,
            out_specs=(vmem, vmem),
            scratch_shapes=scratch,
            compiler_params=pltpu.CompilerParams(
                collective_id=0, has_side_effects=True, vmem_limit_bytes=61 * 1024 * 1024
            ),
        )(*operands)

    return jax.shard_map(
        device_body,
        mesh=mesh,
        in_specs=(seq_spec, seq_spec, wide_spec, wide_spec, square_spec, bias_spec, wide_spec, wide_spec, square_spec, bias_spec),
        out_specs=(out_spec, out_spec),
        check_vma=False,
    )
```

time: 6850 us -> 486 us (0.07)
  waiting for transfers between devices: 5330 us -> 0 us
  blocking collectives: 988 us -> 0 us
  Pallas kernels: 0 us -> 454 us
  matrix products: 277 us -> 0 us
  other arithmetic: 133 us -> 0.01 us
    psum x96 -> x0, waiting for transfers between devices: 5320 us -> none  [the longest x48 2670 us: gru_step(): lax.psum(jnp.dot(gated_row, w_hn, preferred_element_type=jnp.float32), 'r...]
    all_gather x97 -> x0, blocking collectives: 988 us -> none  [the longest x96 945 us: gather_rows(): gathered = lax.all_gather(col_part, 'col', axis=1, tiled=True)]
    pallas_call x0 -> x1, Pallas kernels: none -> 454 us  [device_body(): pl.pallas_call(functools.partial(gru_kernel, dims), name='gru', out_shape...]
    dot_general x144 -> x0, matrix products: 277 us -> none  [the longest x48 192 us: gru_step(): jnp.einsum('bk,kgn->bgn', step_in, w_x, preferred_element_type=jnp.float32)]
  transfers between devices with their start and end apart: 96 -> 0, of which waited for: 96 -> 0; matrix products, arithmetic and copies ran while one was open for 0% -> 0% of each run, Pallas kernels for 0% -> 0%
where the time goes in v1:
time: 486 us
  Pallas kernels  454 us (93%)
  local copies, waits for them, and re-layouts  31.2 us (6%)
    pallas_call x1, Pallas kernels, device_body(): pl.pallas_call(functools.partial(gru_kernel, dims), name='gru', out_shape...  454 us
    slice x2, local copies, waits for them, and re-layouts, device_body(): wru[:, 0]  15.8 us

profile of v1, /device:TPU:97, one launch (start us, length us, event | category | flops | bytes accessed | tf_op | source)
XLA Modules:
  0.0 485.6 jit_solution(7827974360726715994)
XLA Ops:
  0.6 9.5 %fusion = (bf16[720,1,1440]{2,1,0:T(2,128)(2,1)S(1)}, bf16[720,1,1440]{2,1,0:T(2,128)(2,1)S(1)}) fusion(bf16[720,2,1440]{2,1,0:T(2,128)(2,1)} %param.17), kind=kLoop, calls=%fused_computation.4 | loop fusion | bytes 8294400 | tf_op jit(solution)/shard_map/slice | solution.py:422
  10.2 0.0 slice-start
  10.2 0.0 slice-start.1
  10.2 2.7 copy_bitcast_fusion
  12.9 1.6 pad.15.refs_9_
  14.5 0.0 slice-done
  14.5 0.0 slice-done.1
  14.5 6.2 %fusion.1 = (bf16[720,1,1440]{2,1,0:T(2,128)(2,1)S(1)}, bf16[720,1,1440]{2,1,0:T(2,128)(2,1)S(1)}) fusion(bf16[720,2,1440]{2,1,0:T(2,128)(2,1)S(1)} %bitcast.11), kind=kLoop, calls=%fused_computation.5 | loop fusion | bytes 8294400 | tf_op jit(solution)/shard_map/slice | solution.py:422
  20.7 2.6 copy_bitcast_fusion.2
  23.3 0.0 copy-start
  23.3 0.0 copy-start.1
  23.3 1.5 pad.13.refs_4_
  24.8 0.9 copy-done
  25.7 1.6 pad.14.refs_5_
  27.3 0.0 copy-done.1
  27.3 1.6 pad.16.refs_10_
  28.9 453.6 %gru.1 = (bf16[24,16,180]{2,1,0:T(8,128)(2,1)}, f32[2,16,180]{2,1,0:T(8,128)}) custom-call(bf16[24,16,720]{2,1,0:T(8,128)(2,1)} %refs_0_.1, f32[2,16,720]{2,1,0:T(8,128)} %refs_1_.1, bf16[3,720,1440]{2,1,0:T(8,128)(2,1)} %bitcast.12, bf16[720,1440]{1,0:T(8,128)(2,1)} %get-tuple-element.7.refs_3_, bf16[720,1536]{1,0:T(8,128)(2,1)} %pad.13.refs_4_, ...), custom_call_target="tpu_custom_call" | custom-call | tf_op jit(solution)/shard_map/gru/pallas_call | solution.py:471
  482.6 1.6 copy.26
  484.2 1.4 copy.27
  (1 shorter events, 0.0 us)
Async XLA Ops:
  10.2 4.3 slice-start
  10.2 4.3 slice-start.1
  23.3 2.4 copy-start
  23.3 4.0 copy-start.1

commit v2 on v1

--- a/solution.py
+++ b/solution.py
@@ -12,7 +12,7 @@
 BF16 = jnp.bfloat16
 LANES = 128
 
-H1, RH1, H2, RH2 = range(4)
+H1, H2, RH1, RH2 = 0, 2, 4, 5
 R1, N1, R2, N2 = range(4)
 XR, XU, XN, PR, PU, PN, U1, U2 = range(8)
 RING = 4
@@ -22,11 +22,19 @@
     return -(-a // b)
 
 
+def hop(d, n):
+    return min(d, n - d)
+
+
+def nx_hops(nx, ny):
+    return [hop(dx, nx) + hop(dy, ny) for dx in range(nx) for dy in range(ny) if (dx, dy) != (0, 0)]
+
+
 def gru_kernel(dims, *refs):
     steps, batch, rows, cols, nx, ny, chunk = dims
-    (x_hbm, h0, wx1, wru1u, wru1r, wn1, b1, wx2, wru2u, wru2r, wn2, b2,
+    (x_hbm, h0, wx1, wru1, wn1, b1, wx2, wru2, wn2, b2,
      seq_out, fin_out,
-     w_own, w_blk, xb, hcat, h0s, state, ag_src, ag_buf, hs, bias, bpad,
+     w_own, w_blk, w_upd, xb, hcat, h0s, state, ag_buf, hs, bias, bpad,
      p_u1, p_x, p_p, p_u2, s_u1, s_x, s_p, s_u2, xu_keep, pu_keep,
      blk, out_n, out_s, fin_src, fin_buf, fblk, fin_n, fin_s,
      ld_sem, wl_sem, wsend, wrecv, bs_send, bs_recv, x_sem, i_sem,
@@ -49,9 +57,6 @@
     def wait_in(dst, sem):
         pltpu.make_async_copy(dst, dst, sem).wait()
 
-    def hop(d, n):
-        return min(d, n - d)
-
     offsets = [(dx, dy) for dx in range(nx) for dy in range(ny) if (dx, dy) != (0, 0)]
     offsets.sort(key=lambda o: hop(o[0], nx) + hop(o[1], ny))
     dists = [hop(dx, nx) + hop(dy, ny) for dx, dy in offsets]
@@ -67,9 +72,12 @@
         ty = lax.rem(y + d // (2 * nx), ny)
         pl.semaphore_signal(barrier, inc=1, device_id={"row": tr, "col": ty}, device_id_type=MESH)
 
-    moved = ((wru1r, R1), (wn1, N1), (wru2r, R2), (wn2, N2))
-    kept = ((wx1.at[0], XR), (wx1.at[1], XU), (wx1.at[2], XN), (wru1u, U1),
-            (wx2.at[0], PR), (wx2.at[1], PU), (wx2.at[2], PN), (wru2u, U2))
+    moved = ((wru1.at[0], R1), (wn1, N1), (wru2.at[0], R2), (wn2, N2))
+    kept = ((wx1.at[0], XR), (wx1.at[2], XN), (wx1.at[1], XU), (wru1.at[1], U1),
+            (wx2.at[0], PR), (wx2.at[2], PN), (wx2.at[1], PU), (wru2.at[1], U2))
+
+    def block_weight(u):
+        return w_blk.at[u] if u < U1 else w_upd.at[u - U1]
 
     my_rows = pl.ds(pl.multiple_of(device_row * rows, 16), rows)
 
@@ -80,33 +88,46 @@
     def _():
         loads = []
         for src, u in kept:
-            loads.append(pltpu.make_async_copy(src, w_blk.at[u, pl.ds(0, rows)], ld_sem.at[u]))
+            loads.append(pltpu.make_async_copy(src, block_weight(u).at[pl.ds(0, rows)], ld_sem.at[u]))
         xload = pltpu.make_async_copy(x_hbm, xb.at[0], x_sem.at[0])
         xload.start()
         for c in loads:
             c.start()
         pl.semaphore_wait(barrier, 2 * nx * ny - 1)
+
+        @pl.when(x == y)
+        def _():
+            remote(h0, h0s, i_sem.at[0], i_sem.at[1], x, 1, y).start()
+
         for src, u in moved:
             for d in range(nx):
                 tx = wrap(x + d, nx)
                 remote(src.at[:, column_slice(tx)], w_own.at[u, my_rows], wsend.at[u], wrecv.at[u], tx, 1, y).start()
 
-        @pl.when(x == y)
-        def _():
-            remote(h0, h0s, i_sem.at[0], i_sem.at[1], x, 1, y).start()
-
         xload.wait()
         wait_in(xb.at[1], x_sem.at[1])
-        for u in range(8):
-            loads[u].wait()
-            wait_in(w_blk.at[kept[u][1], pl.ds(rows, rows)], bs_recv.at[kept[u][1]])
+
+        def wait_kept(n):
+            loads[n].wait()
+            u = kept[n][1]
+            wait_in(block_weight(u).at[pl.ds(rows, rows)], bs_recv.at[u])
 
         def row_dot(vec, u):
-            return jnp.dot(vec, w_blk[u], preferred_element_type=F32)
+            return jnp.dot(vec, block_weight(u)[:, 0:block], preferred_element_type=F32)
+
+        near_last = sorted(range(nx), key=lambda d: -hop(d, nx))
 
         def spread(src, dst, kind, slot):
-            for d in range(nx):
+            for d in near_last:
                 tx = wrap(x + d, nx)
+                remote(src.at[:, :, column_slice(tx)], dst.at[slot, x], rs_send.at[kind], rs_recv.at[kind, slot], tx, 1, y).start()
+
+        def update_part(vec, u, kept_sum, kept_slot, src, dst, kind, slot):
+            for d in near_last:
+                tx = wrap(x + d, nx)
+                src[0, :, column_slice(tx)] = (
+                    jnp.dot(vec, block_weight(u)[:, column_slice(tx)], preferred_element_type=F32)
+                    + kept_sum[kept_slot, :, column_slice(tx)])
                 remote(src.at[:, :, column_slice(tx)], dst.at[slot, x], rs_send.at[kind], rs_recv.at[kind, slot], tx, 1, y).start()
 
         def spread_wait(src, kind):
@@ -119,50 +140,62 @@
             s_x[0, :, 0:block] = half(XR)
             s_x[1, :, 0:block] = half(XN)
             spread(s_x, p_x, 1, lax.rem(t, RING))
-            xu_keep[...] = half(XU)
+            xu_keep[lax.rem(t, 2), :, 0:block] = half(XU)
 
         s_u1[...] = jnp.zeros_like(s_u1)
         s_u2[...] = jnp.zeros_like(s_u2)
         s_x[...] = jnp.zeros_like(s_x)
         s_p[...] = jnp.zeros_like(s_p)
+        xu_keep[...] = jnp.zeros_like(xu_keep)
+        pu_keep[...] = jnp.zeros_like(pu_keep)
+        for n in range(3):
+            wait_kept(n)
         project(0)
+        spread_wait(s_x, 1)
+        project(1)
+        for n in range(3, 8):
+            wait_kept(n)
 
         def step(i, carry):
-            wait_in(hs.at[0, 0], hs_recv.at[0, lax.rem(i, 2)])
-            h1v = hs[0, lax.rem(i, 2), :, 0:block]
+            @pl.when(i <= steps)
+            def _():
+                wait_in(hs.at[0, 0], hs_recv.at[0, lax.rem(i, RING)])
 
             @pl.when(i < steps)
             def _():
                 @pl.when(i > 0)
                 def _():
                     spread_wait(s_u1, 0)
-                s_u1[0, :, 0:block] = row_dot(h1v, U1) + xu_keep[...]
-                spread(s_u1, p_u1, 0, lax.rem(i, RING))
-
-            @pl.when(i >= 1)
-            def _():
+                update_part(hs[0, lax.rem(i, RING), :, 0:block], U1, xu_keep, lax.rem(i, 2), s_u1, p_u1, 0, lax.rem(i, RING))
+
+            @pl.when(jnp.logical_and(i >= 1, i <= steps))
+            def _():
+                h1v = hs[0, lax.rem(i, RING), :, 0:block]
+
                 @pl.when(i > 1)
                 def _():
                     spread_wait(s_p, 2)
                 s_p[0, :, 0:block] = row_dot(h1v, PR)
                 s_p[1, :, 0:block] = row_dot(h1v, PN)
-                spread(s_p, p_p, 2, lax.rem(i - 1, RING))
-                pu_keep[...] = row_dot(h1v, PU)
-                wait_in(hs.at[1, 0], hs_recv.at[1, lax.rem(i, 2)])
-
-                @pl.when(i > 1)
+                spread(s_p, p_p, 2, lax.rem(i + 3, RING))
+                pu_keep[lax.rem(i + 1, 2), :, 0:block] = row_dot(h1v, PU)
+
+            @pl.when(i >= 2)
+            def _():
+                wait_in(hs.at[1, 0], hs_recv.at[1, lax.rem(i, RING)])
+
+                @pl.when(i > 2)
                 def _():
                     spread_wait(s_u2, 3)
-                s_u2[0, :, 0:block] = row_dot(hs[1, lax.rem(i, 2), :, 0:block], U2) + pu_keep[...]
-                spread(s_u2, p_u2, 3, lax.rem(i - 1, RING))
-
-            @pl.when(i + 1 < steps)
+                update_part(hs[1, lax.rem(i, RING), :, 0:block], U2, pu_keep, lax.rem(i, 2), s_u2, p_u2, 3, lax.rem(i + 2, RING))
+
+            @pl.when(i + 2 < steps)
             def _():
                 spread_wait(s_x, 1)
-                project(i + 1)
+                project(i + 2)
             return carry
 
-        lax.fori_loop(0, steps + 1, step, 0)
+        lax.fori_loop(0, steps + 2, step, 0)
         spread_wait(s_u1, 0)
         spread_wait(s_x, 1)
         spread_wait(s_p, 2)
@@ -186,15 +219,16 @@
         for c in own:
             c.start()
         pl.semaphore_wait(barrier, 2 * nx * ny - 1)
-        remote(x_hbm, xb.at[1], x_sem.at[0], x_sem.at[1], x, 0, y).start()
-        for src, u in kept[:4]:
-            remote(src, w_blk.at[u, pl.ds(rows, rows)], bs_send.at[u], bs_recv.at[u], x, 0, y).start()
-        for src, u in moved:
+
+        def move(src, u):
             for d in range(1, nx):
                 tx = wrap(x + d, nx)
                 remote(src.at[:, column_slice(tx)], w_own.at[u, my_rows], wsend.at[u], wrecv.at[u], tx, 1, y).start()
-        for src, u in kept[4:]:
-            remote(src, w_blk.at[u, pl.ds(rows, rows)], bs_send.at[u], bs_recv.at[u], x, 0, y).start()
+
+        move(*moved[0])
+        remote(x_hbm, xb.at[1], x_sem.at[0], x_sem.at[1], x, 0, y).start()
+        for src, u in kept:
+            remote(src, block_weight(u).at[pl.ds(rows, rows)], bs_send.at[u], bs_recv.at[u], x, 0, y).start()
 
         for u in range(4):
             w_own[u, pl.ds(nx * block, chunk * nx - block)] = jnp.zeros((chunk * nx - block, chunk), BF16)
@@ -225,30 +259,38 @@
             for k in reversed(range(peers)):
                 dx, dy = offsets[k]
                 g = [j for j, (a, b) in enumerate(groups) if a <= k < b][0]
-                remote(ag_src.at[kind], ag_buf.at[kind, k], ag_send.at[kind], ag_recv.at[kind, g],
+                remote(ag_buf.at[kind, 0, 0], ag_buf.at[kind, dy, dx], ag_send.at[kind], ag_recv.at[kind, g],
                        wrap(x + dx, nx), 1, wrap(y + dy, ny)).start()
 
-        def to_blocks(layer, slot):
-            for d in range(ny):
-                remote(ag_src.at[H1 if layer == 0 else H2], hs.at[layer, slot, :, column_slice(x)],
-                       hs_send.at[layer], hs_recv.at[layer, slot], y, 0, wrap(y + d, ny)).start()
+        def to_block(layer, kind, slot):
+            dy = wrap(y - x, ny)
+            for dx in range(nx):
+                remote(ag_buf.at[kind, dy, dx], hs.at[layer, slot, :, column_slice(wrap(x - dx, nx))],
+                       hs_send.at[layer], hs_recv.at[layer, slot], x, 0, y).start()
+
+        def chunks(n):
+            return w_own.at[0, pl.ds(0, n * batch)]
 
         def sent(kind):
-            wait_in(ag_buf.at[kind], ag_send.at[kind])
+            wait_in(chunks(peers), ag_send.at[kind])
 
         def sent_blocks(layer):
-            wait_in(ag_buf.at[0, pl.ds(0, ny)], hs_send.at[layer])
+            wait_in(chunks(nx), hs_send.at[layer])
 
         def weight_rows(dx, dy):
             sx, sy = wrap(x - dx, nx), wrap(y - dy, ny)
             return pl.ds(pl.multiple_of(sy * block + sx * chunk, 32), chunk)
 
+        def arrive(kind, g):
+            a, b = groups[g]
+            wait_in(chunks(b - a), ag_recv.at[kind, g])
+
         def gathered_dot(kind, u, acc):
-            acc = acc + jnp.dot(ag_src[kind], w_own[u, weight_rows(0, 0)], preferred_element_type=F32)
+            acc = acc + jnp.dot(ag_buf[kind, 0, 0], w_own[u, weight_rows(0, 0)], preferred_element_type=F32)
             for g, (a, b) in enumerate(groups):
-                wait_in(ag_buf.at[kind, pl.ds(a, b - a)], ag_recv.at[kind, g])
-                for k in range(a, b):
-                    acc = acc + jnp.dot(ag_buf[kind, k], w_own[u, weight_rows(*offsets[k])], preferred_element_type=F32)
+                arrive(kind, g)
+                for dx, dy in offsets[a:b]:
+                    acc = acc + jnp.dot(ag_buf[kind, dy, dx], w_own[u, weight_rows(dx, dy)], preferred_element_type=F32)
             return acc
 
         def partial_sum(buf, slot, g):
@@ -263,27 +305,27 @@
 
         for layer in range(2):
             kind = H1 if layer == 0 else H2
-            ag_src[kind] = jnp.where(keep, state[layer], 0.0).astype(BF16)
+            ag_buf[kind, 0, 0] = jnp.where(keep, state[layer], 0.0).astype(BF16)
             to_all(kind)
-            to_blocks(layer, layer)
-
-        def copy_row_block():
-            blk[:, column_slice(x)] = ag_src[H2]
-            for k, (dx, dy) in enumerate(offsets):
-                if dy == 0:
-                    blk[:, column_slice(wrap(x - dx, nx))] = ag_buf[H2, k]
-
-        def reset_phase(layer, kind, unit, slot, buf, sem):
+        for src, u in moved[1:]:
+            move(src, u)
+
+        def copy_row_block(kind):
+            blk[:, column_slice(x)] = ag_buf[kind, 0, 0]
+            for dx in range(1, nx):
+                blk[:, column_slice(wrap(x - dx, nx))] = ag_buf[kind, 0, dx]
+
+        def reset_phase(layer, kind, unit, slot, buf, sem, hslot):
             wait_in(buf.at[0], sem)
             pre = gathered_dot(kind, unit, partial_sum(buf, slot, 0) + bias[layer, 0:1])
+            to_block(layer, kind, hslot)
             if layer == 1:
-                copy_row_block()
+                copy_row_block(kind)
             gate = jax.nn.sigmoid(pre)
             out = RH1 if layer == 0 else RH2
-            ag_src[out] = jnp.where(keep, gate * state[layer], 0.0).astype(BF16)
+            ag_buf[out, 0, 0] = jnp.where(keep, gate * state[layer], 0.0).astype(BF16)
             to_all(out)
             sent(kind)
-            sent_blocks(layer)
 
         def candidate_phase(layer, unit, slot, buf, ubuf, usem):
             kind = RH1 if layer == 0 else RH2
@@ -298,61 +340,64 @@
         part = block // (2 * nx)
 
         def step(i, carry):
+            slot1 = lax.rem(i, RING)
+            t2 = i - 2
+            slot2 = lax.rem(i + 2, RING)
+
             @pl.when(i < steps)
             def _():
                 @pl.when(i == 0)
                 def _():
                     wait_weights(R1)
-                slot = lax.rem(i, RING)
-                reset_phase(0, H1, R1, slot, p_x, rs_recv.at[1, slot])
-
-            @pl.when(i >= 2)
-            def _():
-                t = i - 2
-                slot = lax.rem(t, RING)
-
-                @pl.when(i == 2)
-                def _():
-                    wait_weights(N2)
-                new = candidate_phase(1, N2, slot, p_p, p_u2, rs_recv.at[3, slot])
-                sent(RH2)
-
-                @pl.when(t < steps - 1)
-                def _():
-                    ag_src[H2] = new
-                    to_all(H2)
-                    to_blocks(1, lax.rem(t, 2))
-
-            @pl.when(i < steps)
-            def _():
-                @pl.when(i == 0)
-                def _():
-                    wait_weights(N1)
-                slot = lax.rem(i, RING)
-                new = candidate_phase(0, N1, slot, p_x, p_u1, rs_recv.at[0, slot])
-                sent(RH1)
-                ag_src[H1] = new
-
-                @pl.when(i < steps - 1)
-                def _():
-                    to_all(H1)
-                to_blocks(0, lax.rem(i + 1, 2))
-
-            @pl.when(jnp.logical_and(i >= 1, i < steps + 1))
-            def _():
-                @pl.when(i == 1)
+                reset_phase(0, H1 + lax.rem(i, 2), R1, slot1, p_x, rs_recv.at[1, slot1], slot1)
+
+            @pl.when(i == steps)
+            def _():
+                kind = H1 + lax.rem(i, 2)
+                for g in range(len(groups)):
+                    arrive(kind, g)
+                to_block(0, kind, slot1)
+                sent(kind)
+
+            @pl.when(t2 >= 0)
+            def _():
+                @pl.when(t2 == 0)
                 def _():
                     wait_weights(R2)
-                slot = lax.rem(i - 1, RING)
-                reset_phase(1, H2, R2, slot, p_p, rs_recv.at[2, slot])
-
-                @pl.when(i >= 2)
+                reset_phase(1, H2 + lax.rem(i, 2), R2, slot2, p_p, rs_recv.at[2, slot2], slot1)
+
+                @pl.when(t2 >= 1)
                 def _():
                     for k in range(nx):
                         @pl.when(x == k)
                         def _():
-                            out_s[i - 2] = blk[:, 2 * k * part:(2 * k + 1) * part]
-                            out_n[i - 2] = blk[:, (2 * k + 1) * part:(2 * k + 2) * part]
+                            out_s[t2 - 1] = blk[:, 2 * k * part:(2 * k + 1) * part]
+                            out_n[t2 - 1] = blk[:, (2 * k + 1) * part:(2 * k + 2) * part]
+
+            @pl.when(i < steps)
+            def _():
+                @pl.when(i == 0)
+                def _():
+                    wait_weights(N1)
+                new = candidate_phase(0, N1, slot1, p_x, p_u1, rs_recv.at[0, slot1])
+                ag_buf[H1 + lax.rem(i + 1, 2), 0, 0] = new
+                to_all(H1 + lax.rem(i + 1, 2))
+                sent(RH1)
+                sent_blocks(0)
+
+            @pl.when(t2 >= 0)
+            def _():
+                @pl.when(t2 == 0)
+                def _():
+                    wait_weights(N2)
+                new = candidate_phase(1, N2, slot2, p_p, p_u2, rs_recv.at[3, slot2])
+
+                @pl.when(t2 < steps - 1)
+                def _():
+                    ag_buf[H2 + lax.rem(i + 1, 2), 0, 0] = new
+                    to_all(H2 + lax.rem(i + 1, 2))
+                sent(RH2)
+                sent_blocks(1)
             return carry
 
         lax.fori_loop(0, steps + 2, step, 0)
@@ -386,7 +431,7 @@
         for u in range(4):
             wait_in(w_own.at[0, pl.ds(0, (nx - 1) * rows)], wsend.at[u])
         for u in range(8):
-            wait_in(w_blk.at[0, pl.ds(rows, rows)], bs_send.at[u])
+            wait_in(block_weight(u).at[pl.ds(rows, rows)], bs_send.at[u])
 
 
 def solution(mesh):
@@ -404,9 +449,6 @@
         wide = nx * chunk
         part = cols // (2 * nx)
         dims = (steps, batch, rows, cols, nx, ny, chunk)
-
-        def padded(w):
-            return jnp.pad(w, ((0, 0), (0, wide - cols)))
 
         peers = nx * ny - 1
         total_rows = nx * cols
@@ -419,18 +461,19 @@
             if lead:
                 operands += list(lead)
                 specs += [hbm, vmem]
-            operands += [jnp.transpose(wx, (1, 0, 2)), wru[:, 1], padded(wru[:, 0]), padded(wn), b]
-            specs += [hbm, hbm, hbm, hbm, vmem]
+            wru = jnp.pad(jnp.transpose(wru, (1, 0, 2)), ((0, 0), (0, 0), (0, wide - cols)))
+            operands += [jnp.transpose(wx, (1, 0, 2)), wru, jnp.pad(wn, ((0, 0), (0, wide - cols))), b]
+            specs += [hbm, hbm, hbm, vmem]
         scratch = [
             pltpu.VMEM((4, total_rows + wide - cols, chunk), BF16),
-            pltpu.VMEM((8, 2 * rows, cols), BF16),
+            pltpu.VMEM((6, 2 * rows, cols), BF16),
+            pltpu.VMEM((2, 2 * rows, wide), BF16),
             pltpu.VMEM((2, steps, batch, rows), BF16),
             pltpu.VMEM((2, batch, wide), F32),
             pltpu.VMEM((2, batch, rows), F32),
             pltpu.VMEM((2, batch, chunk), F32),
-            pltpu.VMEM((4, batch, chunk), BF16),
-            pltpu.VMEM((4, peers, batch, chunk), BF16),
-            pltpu.VMEM((2, 2, batch, wide), BF16),
+            pltpu.VMEM((6, ny, nx, batch, chunk), BF16),
+            pltpu.VMEM((2, RING, batch, wide), BF16),
             pltpu.VMEM((2, 8, chunk), F32),
             pltpu.VMEM((2, 8, wide), F32),
             pltpu.VMEM((RING, nx, 1, batch, chunk), F32),
@@ -441,8 +484,8 @@
             pltpu.VMEM((2, batch, wide), F32),
             pltpu.VMEM((2, batch, wide), F32),
             pltpu.VMEM((1, batch, wide), F32),
-            pltpu.VMEM((batch, cols), F32),
-            pltpu.VMEM((batch, cols), F32),
+            pltpu.VMEM((2, batch, wide), F32),
+            pltpu.VMEM((2, batch, wide), F32),
             pltpu.VMEM((batch, wide), BF16),
             pltpu.VMEM((steps, batch, part), BF16),
             pltpu.VMEM((steps, batch, part), BF16),
@@ -459,10 +502,10 @@
             dma((8,)),
             dma((2,)),
             dma((4,)),
-            dma((4,)),
-            dma((4, 4)),
+            dma((6,)),
+            dma((6, len(set(nx_hops(nx, ny))))),
             dma((2,)),
-            dma((2, 2)),
+            dma((2, RING)),
             dma((4,)),
             dma((4, RING)),
             dma((2,)),

time: 486 us -> 406 us (0.84)
  Pallas kernels: 454 us -> 389 us
  local copies, waits for them, and re-layouts: 31.2 us -> 15.7 us
    pallas_call x1, Pallas kernels: 454 us -> 389 us  [device_body(): pl.pallas_call(functools.partial(gru_kernel, dims), name='gru', out_shape...]
    slice x2 -> x0, local copies, waits for them, and re-layouts: 15.8 us -> none  [device_body(): wru[:, 0]]
    squeeze x2 -> x0, local copies, waits for them, and re-layouts: 5.27 us -> none  [device_body(): wru[:, 0]]
where the time goes in v2:
time: 406 us
  Pallas kernels  389 us (96%)
  local copies, waits for them, and re-layouts  15.7 us (4%)
    pallas_call x1, Pallas kernels, device_body(): pl.pallas_call(functools.partial(gru_kernel, dims), name='gru', out_shape...  389 us

profile of v2, /device:TPU:97, one launch (start us, length us, event | category | flops | bytes accessed | tf_op | source)
XLA Modules:
  0.0 405.5 jit_solution(13122774427406902284)
XLA Ops:
  0.6 0.0 slice-start
  0.6 3.1 copy.17
  3.7 0.0 slice-start.1
  3.8 2.4 pad.14.refs_3_
  6.2 0.0 slice-done
  6.2 0.0 slice-done.1
  6.2 0.7 copy.16
  6.9 0.0 copy-start
  6.9 2.5 pad.16.refs_7_
  9.3 0.0 copy-done
  9.3 0.0 copy-start.1
  9.4 1.6 pad.15.refs_4_
  11.0 0.8 copy-done.1
  11.8 1.6 pad.17.refs_8_
  13.4 389.1 %gru.1 = (bf16[24,16,180]{2,1,0:T(8,128)(2,1)}, f32[2,16,180]{2,1,0:T(8,128)}) custom-call(bf16[24,16,720]{2,1,0:T(8,128)(2,1)} %refs_0_.1, f32[2,16,720]{2,1,0:T(8,128)} %refs_1_.1, bf16[3,720,1440]{2,1,0:T(8,128)(2,1)} %bitcast.10, bf16[2,720,1536]{2,1,0:T(8,128)(2,1)} %pad.14.refs_3_, bf16[720,1536]{1,0:T(8,128)(2,1)} %pad.15.refs_4_, f32[3,1440]{1,0:T(4,128)} %refs_5_.1, ...), custom_call_target="tpu_custom_call" | custom-call | tf_op jit(solution)/shard_map/gru/pallas_call | solution.py:514
  402.5 1.6 copy.20
  404.2 1.4 copy.21
  (1 shorter events, 0.0 us)
Async XLA Ops:
  0.6 5.5 %slice-start = ((s8[4423680]{0:T(1024)(128)(4,1)}), s8[4194304]{0:T(1024)(128)(4,1)S(1)}, s32[]{:S(2)}) async-start(s8[4423680]{0:T(1024)(128)(4,1)} %bitcast.12), calls=%async_computation | async-start | bytes 8388608
  3.7 2.4 slice-start.1
  6.9 2.5 copy-start
  9.3 2.4 copy-start.1

commit v3 on v2

v3 whole, which is shorter than its diff:
```python
import functools

import jax
import jax.numpy as jnp
from jax import lax
from jax.experimental import pallas as pl
from jax.experimental.pallas import tpu as pltpu
from jax.sharding import PartitionSpec as P

MESH = pl.DeviceIdType.MESH
F32 = jnp.float32
BF16 = jnp.bfloat16
LANES = 128
TILE = 256

STATE, GATED = range(2)
RESET, CAND = range(2)
XR, XU, XN, PR, PU, PN, U1, U2 = range(8)
K_U1, K_X, K_P, K_U2 = range(4)
RING = 4


def hop(d, n):
    return min(d, n - d)


def gru_kernel(dims, *refs):
    steps, batch, rows, nx, ny, chunk = dims
    (x_hbm, h0, wx1, wru1, wn1, b1, wx2, wru2, wn2, b2,
     seq_out, fin_out,
     w_own, w_blk, w_upd, xb, hcat, h0s, state, ag_buf, hs, bias, bpad,
     p_in, p_upd, s_u1, s_x, s_p, s_u2, xu_keep, pu_keep,
     blk, out_own, out_s, out_far, fin_buf, fblk, fin_n, fin_s, last_s,
     ld_sem, wl_sem, wsend, wrecv, bs_send, bs_recv, x_sem, i_sem,
     ag_send, ag_recv, hs_send, hs_recv, rs_send, in_recv, upd_recv, f_sem, o_send, o_recv, d_sem) = refs
    block = 2 * rows
    half = nx // 2
    part = block // (2 * nx)
    device_row = lax.axis_index("row")
    y = lax.axis_index("col")
    x = device_row // 2
    core = lax.rem(device_row, 2)

    def wrap(v, n):
        return lax.rem(v + n, n)

    def remote(src, dst, ssem, rsem, tx, tc, ty):
        return pltpu.make_async_remote_copy(
            src_ref=src, dst_ref=dst, send_sem=ssem, recv_sem=rsem,
            device_id={"row": tx * 2 + tc, "col": ty}, device_id_type=MESH,
        )

    def wait_in(dst, sem):
        pltpu.make_async_copy(dst, dst, sem).wait()

    def column_slice(i):
        return pl.ds(pl.multiple_of(i * chunk, LANES), chunk)

    barrier = pltpu.get_barrier_semaphore()
    for d in range(1, 2 * nx * ny):
        tr = lax.rem(device_row + d % (2 * nx), 2 * nx)
        ty = lax.rem(y + d // (2 * nx), ny)
        pl.semaphore_signal(barrier, inc=1, device_id={"row": tr, "col": ty}, device_id_type=MESH)

    moved = {RESET: (wru1.at[0], wru2.at[0]), CAND: (wn1, wn2)}
    kept = ((wx1.at[0], XR), (wx1.at[2], XN), (wx1.at[1], XU), (wru1.at[1], U1),
            (wx2.at[0], PR), (wx2.at[2], PN), (wx2.at[1], PU), (wru2.at[1], U2))
    my_rows = pl.ds(pl.multiple_of(device_row * rows, 16), rows)

    def block_weight(u):
        return w_blk.at[u] if u < U1 else w_upd.at[u - U1]

    def move(u, offsets):
        for d in offsets:
            tx = wrap(x + d, nx)
            for layer in range(2):
                @pl.when(tx // half == layer)
                def _():
                    remote(moved[u][layer].at[:, column_slice(lax.rem(tx, half))], w_own.at[u, my_rows],
                           wsend.at[u], wrecv.at[u], tx, 1, y).start()

    @pl.when(core == 0)
    def _():
        loads = []
        for src, u in kept:
            loads.append(pltpu.make_async_copy(src, block_weight(u).at[pl.ds(0, rows)], ld_sem.at[u]))
        xload = pltpu.make_async_copy(x_hbm, xb.at[0], x_sem.at[0])
        xload.start()
        for c in loads:
            c.start()
        pl.semaphore_wait(barrier, 2 * nx * ny - 1)

        @pl.when(x == y)
        def _():
            remote(h0, h0s, i_sem.at[0], i_sem.at[1], x, 1, y).start()

        move(RESET, range(nx))
        for ref in (s_u1, s_u2, s_x, s_p, xu_keep, pu_keep):
            ref[...] = jnp.zeros_like(ref)
        xload.wait()
        wait_in(xb.at[1], x_sem.at[1])

        def wait_kept(n):
            loads[n].wait()
            u = kept[n][1]
            wait_in(block_weight(u).at[pl.ds(rows, rows)], bs_recv.at[u])

        def row_dot(vec, u):
            return jnp.dot(vec, block_weight(u)[:, 0:block], preferred_element_type=F32)

        def owners(layer):
            xs = lax.rem(x, half)
            first = jnp.where(x // half == layer, lax.rem(xs + 1, half), xs)
            return [lax.rem(first + j, half) for j in range(half)]

        def send_part(src, dst, kind, layer, slot, j, rsem):
            remote(src.at[:, :, column_slice(j)], dst.at[slot, x], rs_send.at[kind], rsem.at[slot], layer * half + j, 1, y).start()

        def spread(src, kind, layer, slot):
            for j in owners(layer):
                send_part(src, p_in, kind, layer, slot, j, in_recv)

        def spread_wait(src, kind):
            wait_in(src, rs_send.at[kind])

        def update_part(vec, u, kept_sum, kept_slot, src, kind, layer, slot):
            for j in owners(layer):
                src[0, :, column_slice(j)] = (
                    jnp.dot(vec, block_weight(u)[:, column_slice(j)], preferred_element_type=F32)
                    + kept_sum[kept_slot, :, column_slice(j)])
                send_part(src, p_upd, kind, layer, slot, j, upd_recv)

        def project(t):
            def rows_of(g):
                return (jnp.dot(xb[0, t], w_blk[g, 0:rows], preferred_element_type=F32)
                        + jnp.dot(xb[1, t], w_blk[g, rows:block], preferred_element_type=F32))
            s_x[0, :, 0:block] = rows_of(XR)
            s_x[1, :, 0:block] = rows_of(XN)
            spread(s_x, K_X, 0, lax.rem(t, RING))
            xu_keep[lax.rem(t, 2), :, 0:block] = rows_of(XU)

        def state_block(layer, slot):
            return hs[layer, slot, :, 0:block]

        def first_update(i):
            update_part(state_block(0, lax.rem(i, RING)), U1, xu_keep, lax.rem(i, 2), s_u1, K_U1, 0, lax.rem(i, RING))

        for n in range(3):
            wait_kept(n)
        project(0)
        spread_wait(s_x, K_X)
        project(1)
        for n in range(3, 8):
            wait_kept(n)
        wait_in(hs.at[0, 0], hs_recv.at[0, 0])
        first_update(0)
        move(CAND, range(nx))

        def step(i, carry):
            @pl.when(jnp.logical_and(i >= 1, i <= steps))
            def _():
                wait_in(hs.at[0, 0], hs_recv.at[0, lax.rem(i, RING)])

                @pl.when(i < steps)
                def _():
                    spread_wait(s_u1, K_U1)
                    first_update(i)

                h1v = state_block(0, lax.rem(i, RING))

                @pl.when(i > 1)
                def _():
                    spread_wait(s_p, K_P)
                s_p[0, :, 0:block] = row_dot(h1v, PR)
                s_p[1, :, 0:block] = row_dot(h1v, PN)
                spread(s_p, K_P, 1, lax.rem(i + 3, RING))
                pu_keep[lax.rem(i + 1, 2), :, 0:block] = row_dot(h1v, PU)

            @pl.when(i >= 2)
            def _():
                wait_in(hs.at[1, 0], hs_recv.at[1, lax.rem(i + 2, RING)])

                @pl.when(i > 2)
                def _():
                    spread_wait(s_u2, K_U2)
                update_part(state_block(1, lax.rem(i + 2, RING)), U2, pu_keep, lax.rem(i, 2), s_u2, K_U2, 1, lax.rem(i + 2, RING))

            @pl.when(i + 2 < steps)
            def _():
                spread_wait(s_x, K_X)
                project(i + 2)
            return carry

        lax.fori_loop(0, steps + 2, step, 0)
        spread_wait(s_u1, K_U1)
        spread_wait(s_x, K_X)
        spread_wait(s_p, K_P)
        spread_wait(s_u2, K_U2)
        for u in range(2):
            wait_in(w_own.at[0, pl.ds(0, nx * rows)], wsend.at[u])

        @pl.when(x == y)
        def _():
            wait_in(h0, i_sem.at[0])
        wait_in(out_own.at[pl.ds(0, steps - 1)], o_recv)
        wait_in(fin_s, d_sem.at[1])
        wait_in(last_s, d_sem.at[3])
        seq_out[pl.ds(0, steps - 1)] = out_own[pl.ds(0, steps - 1)]
        seq_out[steps - 1] = last_s[...]
        fin_out[...] = fin_s[...]

    @pl.when(core == 1)
    def _():
        layer = x // half
        xs = lax.rem(x, half)
        other = nx - 1 - x
        for u in range(2):
            for l in range(2):
                @pl.when(layer == l)
                def _():
                    pltpu.make_async_copy(moved[u][l].at[:, column_slice(xs)], w_own.at[u, my_rows], wl_sem.at[u]).start()
        pl.semaphore_wait(barrier, 2 * nx * ny - 1)

        @pl.when(x == y)
        def _():
            wait_in(h0s, i_sem.at[1])
            hcat[...] = jnp.zeros_like(hcat)
            hcat[:, :, 0:rows] = h0s[...]
            hcat[:, :, rows:block] = h0[...]
            for d in range(1, nx):
                tx = wrap(x + d, nx)
                remote(hcat.at[tx // half, :, column_slice(lax.rem(tx, half))], state, i_sem.at[2], i_sem.at[3], tx, 1, y).start()
            state[...] = hcat[layer, :, column_slice(xs)]

        move(RESET, range(1, nx))
        remote(x_hbm, xb.at[1], x_sem.at[0], x_sem.at[1], x, 0, y).start()
        for src, u in kept:
            remote(src, block_weight(u).at[pl.ds(rows, rows)], bs_send.at[u], bs_recv.at[u], x, 0, y).start()

        offsets = [(dx, dy) for dx in range(half) for dy in range(ny) if (dx, dy) != (0, 0)]
        offsets.sort(key=lambda o: (o[0], hop(o[1], ny)))
        peers = len(offsets)
        groups = ((0, 2), (2, 4), (4, 7))
        across = [o for o in reversed(offsets) if o[0]]
        along = [o for o in reversed(offsets) if not o[0]]
        send_order = []
        while across or along:
            send_order += [q.pop(0) for q in (across, along) if q]
        pad = half * chunk - block
        for u in range(2):
            w_own[u, pl.ds(ny * block, pad)] = jnp.zeros((pad, chunk), BF16)
        bpad[...] = jnp.zeros_like(bpad)
        for l, b in enumerate((b1, b2)):
            @pl.when(layer == l)
            def _():
                bpad[0:3, 0:block] = b[...]
        bias[...] = bpad[:, column_slice(xs)]
        valid = jnp.minimum(block - xs * chunk, chunk)
        keep = lax.broadcasted_iota(jnp.int32, (batch, chunk), 1) < valid

        def to_all(kind):
            for dx, dy in send_order:
                k = offsets.index((dx, dy))
                g = [j for j, (a, b) in enumerate(groups) if a <= k < b][0]
                remote(ag_buf.at[kind, 0, 0], ag_buf.at[kind, dy, dx], ag_send.at[kind], ag_recv.at[kind, g],
                       layer * half + lax.rem(xs + dx, half), 1, wrap(y + dy, ny)).start()

        def to_blocks(slot):
            for d in sorted(range(ny), key=lambda d: -hop(d, ny)):
                remote(ag_buf.at[STATE, 0, 0], hs.at[layer, slot, :, column_slice(xs)],
                       hs_send, hs_recv.at[layer, slot], y, 0, wrap(y + d, ny)).start()

        def chunks(n):
            return w_own.at[0, pl.ds(0, n * batch)]

        def states(n):
            return p_in.at[0, pl.ds(0, n), 0]

        def weight_rows(dx, dy):
            sx, sy = wrap(xs - dx, half), wrap(y - dy, ny)
            return pl.ds(pl.multiple_of(sy * block + sx * chunk, 32), chunk)

        def arrive(kind, g):
            a, b = groups[g]
            wait_in(chunks(b - a), ag_recv.at[kind, g])

        def gathered_dot(kind, u, acc):
            cols = [acc[:, n * TILE:(n + 1) * TILE] for n in range(3)]

            def add(group):
                sums = [None] * 4
                for c, (dx, dy) in enumerate(group):
                    vec = ag_buf[kind, dy, dx]
                    for n in (0, 1, 2 + c % 2):
                        col = min(n, 2)
                        out = jnp.dot(vec, w_own[u, weight_rows(dx, dy), col * TILE:(col + 1) * TILE], preferred_element_type=F32)
                        sums[n] = out if sums[n] is None else sums[n] + out
                for n, v in enumerate(sums):
                    if v is not None:
                        cols[min(n, 2)] = cols[min(n, 2)] + v

            add([(0, 0)])
            for g, (a, b) in enumerate(groups):
                arrive(kind, g)
                add(offsets[a:b])
            return jnp.concatenate(cols, axis=1)

        def partial_sum(buf, slot, g):
            total = buf[slot, 0, g]
            for s in range(1, nx):
                total = total + buf[slot, s, g]
            return total

        def wait_weights(u):
            wait_in(w_own.at[u, pl.ds(0, rows)], wl_sem.at[u])
            wait_in(w_own.at[u, pl.ds(0, (2 * nx - 1) * rows)], wrecv.at[u])

        def take_outputs(t):
            for dx in range(half):
                blk[:, column_slice(wrap(xs - dx, half))] = ag_buf[STATE, 0, dx]
            for k in range(half, nx):
                @pl.when(x == k)
                def _():
                    o = nx - 1 - k
                    out_s[t] = blk[:, 2 * k * part:(2 * k + 1) * part]
                    out_own[t] = blk[:, (2 * k + 1) * part:(2 * k + 2) * part]
                    out_far[0, t] = blk[:, 2 * o * part:(2 * o + 1) * part]
                    out_far[1, t] = blk[:, (2 * o + 1) * part:(2 * o + 2) * part]

        done = pl.ds(0, steps - 1)

        def outputs():
            return ((out_s, 0, x), (out_far.at[0], 0, other), (out_far.at[1], 1, other))

        @pl.when(x != y)
        def _():
            wait_in(state, i_sem.at[3])
        ag_buf[STATE, 0, 0] = jnp.where(keep, state[...], 0.0).astype(BF16)
        to_blocks(0)
        to_all(STATE)
        move(CAND, range(1, nx))

        def phase(n, carry):
            t = n // 2
            p = lax.rem(n, 2)
            slot = lax.rem(t, RING)

            @pl.when(t == 0)
            def _():
                wait_weights(p)

            @pl.when(p == RESET)
            def _():
                wait_in(p_in.at[0], in_recv.at[slot])
            pre = gathered_dot(p, p, partial_sum(p_in, slot, p) + bias[pl.ds(2 * p, 1)])

            @pl.when(p == RESET)
            def _():
                @pl.when(jnp.logical_and(layer == 1, t >= 1))
                def _():
                    take_outputs(t - 1)
                gated = jax.nn.sigmoid(pre) * state[...]
                ag_buf[GATED, 0, 0] = jnp.where(keep, gated, 0.0).astype(BF16)
                to_all(GATED)
                wait_in(chunks(peers), ag_send.at[STATE])
                wait_in(chunks(ny), hs_send)

                @pl.when(jnp.logical_and(layer == 1, t == steps - 1))
                def _():
                    for n, (src, tc, tx) in enumerate(outputs()):
                        remote(src.at[done], out_own.at[done], o_send.at[n], o_recv, tx, tc, y).start()

            @pl.when(p == CAND)
            def _():
                cand = jnp.tanh(pre)
                wait_in(p_upd.at[0], upd_recv.at[slot])
                upd = jax.nn.sigmoid(partial_sum(p_upd, slot, 0) + bias[1:2])
                new = (1.0 - upd) * cand + upd * state[...]
                state[...] = new
                ag_buf[STATE, 0, 0] = jnp.where(keep, new, 0.0).astype(BF16)

                @pl.when(t < steps - 1)
                def _():
                    to_all(STATE)

                @pl.when(jnp.logical_or(layer == 0, t < steps - 1))
                def _():
                    to_blocks(lax.rem(t + 1, RING))

                wait_in(chunks(peers), ag_send.at[GATED])
            return carry

        lax.fori_loop(0, 2 * steps, phase, 0)

        for d in range(1, nx):
            tx = wrap(x + d, nx)
            remote(state, fin_buf.at[layer, xs], f_sem.at[0], f_sem.at[1], tx, 1, y).start()
        fin_buf[layer, xs] = state[...]
        wait_in(states(nx - 1), f_sem.at[1])
        for l in range(2):
            for j in range(half):
                fblk[l, :, j * chunk:(j + 1) * chunk] = fin_buf[l, j]
        for k in range(nx):
            @pl.when(x == k)
            def _():
                s_part = fblk[:, :, 2 * k * part:(2 * k + 1) * part]
                n_part = fblk[:, :, (2 * k + 1) * part:(2 * k + 2) * part]
                fin_s[...] = s_part
                fin_n[...] = n_part
                last_s[...] = s_part[1].astype(BF16)
                seq_out[steps - 1] = n_part[1].astype(BF16)
        remote(last_s, last_s, d_sem.at[2], d_sem.at[3], x, 0, y).start()
        remote(fin_s, fin_s, d_sem.at[0], d_sem.at[1], x, 0, y).start()

        @pl.when(layer == 0)
        def _():
            wait_in(out_own.at[done], o_recv)
            wait_in(chunks(ny), hs_send)

        @pl.when(layer == 1)
        def _():
            for n, (src, tc, tx) in enumerate(outputs()):
                wait_in(src.at[done], o_send.at[n])
        seq_out[done] = out_own[done]
        fin_out[...] = fin_n[...]
        wait_in(last_s, d_sem.at[2])
        wait_in(fin_s, d_sem.at[0])
        wait_in(states(nx - 1), f_sem.at[0])

        @pl.when(x == y)
        def _():
            wait_in(states(nx - 1), i_sem.at[2])
        wait_in(xb.at[1], x_sem.at[0])
        for u in range(2):
            wait_in(w_own.at[0, pl.ds(0, (nx - 1) * rows)], wsend.at[u])
        for u in range(8):
            wait_in(block_weight(u).at[pl.ds(rows, rows)], bs_send.at[u])


def solution(mesh):
    nx, ny = mesh.shape["row"] // 2, mesh.shape["col"]
    half = nx // 2
    seq_spec = P(None, "data", "row")
    out_spec = P(None, "data", ("col", "row"))
    wide_spec = P("row", None, "col")
    square_spec = P("row", "col")
    bias_spec = P(None, "col")

    def device_body(x_rows, h_rows, wx_l1, whru_l1, whn_l1, bias_l1, wx_l2, whru_l2, whn_l2, bias_l2):
        steps, batch, rows = x_rows.shape
        cols = whn_l1.shape[1]
        chunk = -(-cols // (half * LANES)) * LANES
        wide = half * chunk
        part = cols // (2 * nx)
        dims = (steps, batch, rows, nx, ny, chunk)
        groups = 1 + max(hop(dx, nx) + hop(dy, ny) for dx in range(half) for dy in range(ny))

        hbm = pl.BlockSpec(memory_space=pl.ANY)
        vmem = pl.BlockSpec(memory_space=pltpu.VMEM)
        dma = pltpu.SemaphoreType.DMA
        operands = [x_rows, h_rows]
        specs = [hbm, vmem]
        for wx, wru, wn, b in ((wx_l1, whru_l1, whn_l1, bias_l1), (wx_l2, whru_l2, whn_l2, bias_l2)):
            wru = jnp.pad(jnp.transpose(wru, (1, 0, 2)), ((0, 0), (0, 0), (0, wide - cols)))
            operands += [jnp.transpose(wx, (1, 0, 2)), wru, jnp.pad(wn, ((0, 0), (0, wide - cols))), b]
            specs += [hbm, hbm, hbm, vmem]
        scratch = [
            pltpu.VMEM((2, ny * cols + wide - cols, chunk), BF16),
            pltpu.VMEM((6, 2 * rows, cols), BF16),
            pltpu.VMEM((2, 2 * rows, wide), BF16),
            pltpu.VMEM((2, steps, batch, rows), BF16),
            pltpu.VMEM((2, batch, wide), F32),
            pltpu.VMEM((2, batch, rows), F32),
            pltpu.VMEM((batch, chunk), F32),
            pltpu.VMEM((2, ny, half, batch, chunk), BF16),
            pltpu.VMEM((2, RING, batch, wide), BF16),
            pltpu.VMEM((8, chunk), F32),
            pltpu.VMEM((8, wide), F32),
            pltpu.VMEM((RING, nx, 2, batch, chunk), F32),
            pltpu.VMEM((RING, nx, 1, batch, chunk), F32),
            pltpu.VMEM((1, batch, wide), F32),
            pltpu.VMEM((2, batch, wide), F32),
            pltpu.VMEM((2, batch, wide), F32),
            pltpu.VMEM((1, batch, wide), F32),
            pltpu.VMEM((2, batch, wide), F32),
            pltpu.VMEM((2, batch, wide), F32),
            pltpu.VMEM((batch, wide), BF16),
            pltpu.VMEM((steps, batch, part), BF16),
            pltpu.VMEM((steps, batch, part), BF16),
            pltpu.VMEM((2, steps, batch, part), BF16),
            pltpu.VMEM((2, half, batch, chunk), F32),
            pltpu.VMEM((2, batch, wide), F32),
            pltpu.VMEM((2, batch, part), F32),
            pltpu.VMEM((2, batch, part), F32),
            pltpu.VMEM((batch, part), BF16),
            dma((8,)),
            dma((2,)),
            dma((2,)),
            dma((2,)),
            dma((8,)),
            dma((8,)),
            dma((2,)),
            dma((4,)),
            dma((2,)),
            dma((2, groups)),
            dma(()),
            dma((2, RING)),
            dma((4,)),
            dma((RING,)),
            dma((RING,)),
            dma((2,)),
            dma((3,)),
            dma(()),
            dma((4,)),
        ]
        return pl.pallas_call(
            functools.partial(gru_kernel, dims),
            name="gru",
            out_shape=(
                jax.ShapeDtypeStruct((steps, batch, part), BF16),
                jax.ShapeDtypeStruct((2, batch, part), F32),
            ),
            in_specs=specs,
            out_specs=(vmem, vmem),
            scratch_shapes=scratch,
            compiler_params=pltpu.CompilerParams(
                collective_id=0, has_side_effects=True, vmem_limit_bytes=61 * 1024 * 1024
            ),
        )(*operands)

    return jax.shard_map(
        device_body,
        mesh=mesh,
        in_specs=(seq_spec, seq_spec, wide_spec, wide_spec, square_spec, bias_spec, wide_spec, wide_spec, square_spec, bias_spec),
        out_specs=(out_spec, out_spec),
        check_vma=False,
    )
```

time: 406 us -> 401 us (0.988)
  Pallas kernels: 389 us -> 384 us
    pallas_call x1, Pallas kernels: 389 us -> 384 us  [device_body(): pl.pallas_call(functools.partial(gru_kernel, dims), name='gru', out_shape...]
where the time goes in v3:
time: 401 us
  Pallas kernels  384 us (96%)
  local copies, waits for them, and re-layouts  15.7 us (4%)
    pallas_call x1, Pallas kernels, device_body(): pl.pallas_call(functools.partial(gru_kernel, dims), name='gru', out_shape...  384 us

profile of v3, /device:TPU:97, one launch (start us, length us, event | category | flops | bytes accessed | tf_op | source)
XLA Modules:
  0.0 400.6 jit_solution(16762324903135029169)
XLA Ops:
  0.6 0.0 slice-start
  0.6 3.1 copy.17
  3.7 0.0 slice-start.1
  3.8 2.4 pad.14.refs_3_
  6.2 0.0 slice-done
  6.2 0.0 slice-done.1
  6.2 0.7 copy.16
  6.9 0.0 copy-start
  6.9 2.5 pad.16.refs_7_
  9.3 0.0 copy-done
  9.3 0.0 copy-start.1
  9.4 1.6 pad.15.refs_4_
  11.0 0.8 copy-done.1
  11.8 1.6 pad.17.refs_8_
  13.4 384.2 %gru.1 = (bf16[24,16,180]{2,1,0:T(8,128)(2,1)}, f32[2,16,180]{2,1,0:T(8,128)}) custom-call(bf16[24,16,720]{2,1,0:T(8,128)(2,1)} %refs_0_.1, f32[2,16,720]{2,1,0:T(8,128)} %refs_1_.1, bf16[3,720,1440]{2,1,0:T(8,128)(2,1)} %bitcast.10, bf16[2,720,1536]{2,1,0:T(8,128)(2,1)} %pad.14.refs_3_, bf16[720,1536]{1,0:T(8,128)(2,1)} %pad.15.refs_4_, f32[3,1440]{1,0:T(4,128)} %refs_5_.1, ...), custom_call_target="tpu_custom_call" | custom-call | tf_op jit(solution)/shard_map/gru/pallas_call | solution.py:516
  397.6 1.6 copy.20
  399.2 1.4 copy.21
  (1 shorter events, 0.0 us)
Async XLA Ops:
  0.6 5.5 %slice-start = ((s8[4423680]{0:T(1024)(128)(4,1)}), s8[4194304]{0:T(1024)(128)(4,1)S(1)}, s32[]{:S(2)}) async-start(s8[4423680]{0:T(1024)(128)(4,1)} %bitcast.12), calls=%async_computation | async-start | bytes 8388608
  3.7 2.4 slice-start.1
  6.9 2.5 copy-start
  9.3 2.4 copy-start.1

commit v4 on v2

--- a/solution.py
+++ b/solution.py
@@ -36,9 +36,9 @@
      seq_out, fin_out,
      w_own, w_blk, w_upd, xb, hcat, h0s, state, ag_buf, hs, bias, bpad,
      p_u1, p_x, p_p, p_u2, s_u1, s_x, s_p, s_u2, xu_keep, pu_keep,
-     blk, out_n, out_s, fin_src, fin_buf, fblk, fin_n, fin_s,
-     ld_sem, wl_sem, wsend, wrecv, bs_send, bs_recv, x_sem, i_sem,
-     ag_send, ag_recv, hs_send, hs_recv, rs_send, rs_recv, f_sem, o_sem) = refs
+     raw, raw_n, tail, blk, out_n, out_s, fin_src, fin_buf, fblk, fin_n, fin_s,
+     raw_sem, ld_sem, wl_sem, wsend, wrecv, pr_send, pr_recv, bs_send, bs_recv, x_sem, i_sem,
+     ag_send, ag_recv, hs_send, hs_recv, rs_send, rs_recv, in_recv, f_sem, o_sem) = refs
     block = 2 * rows
     device_row = lax.axis_index("row")
     y = lax.axis_index("col")
@@ -72,9 +72,9 @@
         ty = lax.rem(y + d // (2 * nx), ny)
         pl.semaphore_signal(barrier, inc=1, device_id={"row": tr, "col": ty}, device_id_type=MESH)
 
-    moved = ((wru1.at[0], R1), (wn1, N1), (wru2.at[0], R2), (wn2, N2))
-    kept = ((wx1.at[0], XR), (wx1.at[2], XN), (wx1.at[1], XU), (wru1.at[1], U1),
-            (wx2.at[0], PR), (wx2.at[2], PN), (wx2.at[1], PU), (wru2.at[1], U2))
+    kept = ((wx1.at[0], XR), (wx1.at[2], XN), (wx1.at[1], XU), (None, U1),
+            (wx2.at[0], PR), (wx2.at[2], PN), (wx2.at[1], PU), (None, U2))
+    main = (block - (nx - 1) * chunk) // LANES * LANES
 
     def block_weight(u):
         return w_blk.at[u] if u < U1 else w_upd.at[u - U1]
@@ -84,32 +84,96 @@
     def column_slice(i):
         return pl.ds(pl.multiple_of(i * chunk, LANES), chunk)
 
+    size = raw.shape[1]
+    jobs = [(l, n) for l in range(2) for n in range(rows // size)]
+
+    def fetch(srcs, buf, sem, k):
+        l, n = jobs[k]
+        return pltpu.make_async_copy(srcs[l].at[pl.ds(n * size, size)], buf.at[k % 2], raw_sem.at[sem, k % 2])
+
+    def fetch_first():
+        for k in range(2):
+            fetch((wru1, wru2), raw, 0, k).start()
+            fetch((wn1, wn2), raw_n, 1, k).start()
+
+    def split_gates(put):
+        for k, (l, n) in enumerate(jobs):
+            fetch((wru1, wru2), raw, 0, k).wait()
+
+            def some(m, carry):
+                both = jnp.transpose(raw[k % 2, pl.ds(pl.multiple_of(m * 16, 16), 16)], (1, 0, 2))
+                put(l, n * size + m * 16, both[0], both[1])
+                return carry
+            lax.fori_loop(0, size // 16, some, 0)
+            if k + 2 < len(jobs):
+                fetch((wru1, wru2), raw, 0, k + 2).start()
+            fetch((wn1, wn2), raw_n, 1, k).wait()
+            rest = raw_n[k % 2, :, (nx - 1) * chunk + main:]
+            tail[l, pl.ds(n * size, size)] = jnp.concatenate([rest, jnp.zeros((size, LANES - rest.shape[1]), BF16)], axis=1)
+            if k + 2 < len(jobs):
+                fetch((wn1, wn2), raw_n, 1, k + 2).start()
+
+    def pieces(u, j, reset_source):
+        l = 0 if u in (R1, N1) else 1
+        if u in (R1, R2):
+            return [(reset_source(l, j), pl.ds(0, chunk))]
+        src = (wn1, wn2)[l]
+        if j < nx - 1:
+            return [(src.at[:, pl.ds(j * chunk, chunk)], pl.ds(0, chunk))]
+        return [(src.at[:, pl.ds(j * chunk, main)], pl.ds(0, main)), (tail.at[l], pl.ds(main, LANES))]
+
+    def move(u, reset_source, to_self):
+        for tx in range(nx):
+            for src, lanes in pieces(u, tx, reset_source):
+                dst = w_own.at[u, my_rows, lanes]
+                if to_self is None:
+                    remote(src, dst, wsend.at[u], wrecv.at[u], tx, 1, y).start()
+                else:
+                    @pl.when(x != tx)
+                    def _():
+                        remote(src, dst, wsend.at[u], wrecv.at[u], tx, 1, y).start()
+
+                    @pl.when(x == tx)
+                    def _():
+                        pltpu.make_async_copy(src, dst, to_self.at[u]).start()
+
     @pl.when(core == 0)
     def _():
-        loads = []
-        for src, u in kept:
-            loads.append(pltpu.make_async_copy(src, block_weight(u).at[pl.ds(0, rows)], ld_sem.at[u]))
+        partner_rows = pl.ds(pl.multiple_of((device_row + 1) * rows, 16), rows)
+        fetch_first()
+        spare = lambda l, j: (nx * l + j) * rows
+        w_upd[:, pl.ds(0, rows), pl.ds(nx * chunk - LANES, LANES)] = jnp.zeros((2, rows, LANES), BF16)
+        for l in range(2):
+            w_own[0, pl.ds(spare(l, nx - 1), rows), pl.ds(chunk - LANES, LANES)] = jnp.zeros((rows, LANES), BF16)
+
+        def put(l, row, reset, update):
+            w_upd[l, pl.ds(pl.multiple_of(row, 16), 16), 0:block] = update
+            for j in range(nx):
+                width = min(chunk, block - j * chunk)
+                w_own[0, pl.ds(pl.multiple_of(spare(l, j) + row, 16), 16), 0:width] = reset[:, j * chunk:j * chunk + width]
+
+        split_gates(put)
+        reset_rows = lambda l, j: w_own.at[0, pl.ds(spare(l, j), rows)]
         xload = pltpu.make_async_copy(x_hbm, xb.at[0], x_sem.at[0])
         xload.start()
-        for c in loads:
-            c.start()
+        for src, u in kept:
+            if src is not None:
+                pltpu.make_async_copy(src, block_weight(u).at[pl.ds(0, rows)], ld_sem.at[u]).start()
         pl.semaphore_wait(barrier, 2 * nx * ny - 1)
 
         @pl.when(x == y)
         def _():
             remote(h0, h0s, i_sem.at[0], i_sem.at[1], x, 1, y).start()
 
-        for src, u in moved:
-            for d in range(nx):
-                tx = wrap(x + d, nx)
-                remote(src.at[:, column_slice(tx)], w_own.at[u, my_rows], wsend.at[u], wrecv.at[u], tx, 1, y).start()
+        move(R1, reset_rows, None)
 
         xload.wait()
         wait_in(xb.at[1], x_sem.at[1])
 
         def wait_kept(n):
-            loads[n].wait()
             u = kept[n][1]
+            if u < U1:
+                wait_in(block_weight(u).at[pl.ds(0, rows)], ld_sem.at[u])
             wait_in(block_weight(u).at[pl.ds(rows, rows)], bs_recv.at[u])
 
         def row_dot(vec, u):
@@ -117,10 +181,10 @@
 
         near_last = sorted(range(nx), key=lambda d: -hop(d, nx))
 
-        def spread(src, dst, kind, slot):
+        def spread(src, dst, g, kind, slot):
             for d in near_last:
                 tx = wrap(x + d, nx)
-                remote(src.at[:, :, column_slice(tx)], dst.at[slot, x], rs_send.at[kind], rs_recv.at[kind, slot], tx, 1, y).start()
+                remote(src.at[g, :, column_slice(tx)], dst.at[slot, x, g], rs_send.at[kind], in_recv.at[kind - 1, slot, g], tx, 1, y).start()
 
         def update_part(vec, u, kept_sum, kept_slot, src, dst, kind, slot):
             for d in near_last:
@@ -137,9 +201,9 @@
             def half(g):
                 return (jnp.dot(xb[0, t], w_blk[g, 0:rows], preferred_element_type=F32)
                         + jnp.dot(xb[1, t], w_blk[g, rows:block], preferred_element_type=F32))
-            s_x[0, :, 0:block] = half(XR)
-            s_x[1, :, 0:block] = half(XN)
-            spread(s_x, p_x, 1, lax.rem(t, RING))
+            for g, u in enumerate((XR, XN)):
+                s_x[g, :, 0:block] = half(u)
+                spread(s_x, p_x, g, 1, lax.rem(t, RING))
             xu_keep[lax.rem(t, 2), :, 0:block] = half(XU)
 
         s_u1[...] = jnp.zeros_like(s_u1)
@@ -151,6 +215,7 @@
         for n in range(3):
             wait_kept(n)
         project(0)
+        move(N1, reset_rows, None)
         spread_wait(s_x, 1)
         project(1)
         for n in range(3, 8):
@@ -175,9 +240,9 @@
                 @pl.when(i > 1)
                 def _():
                     spread_wait(s_p, 2)
-                s_p[0, :, 0:block] = row_dot(h1v, PR)
-                s_p[1, :, 0:block] = row_dot(h1v, PN)
-                spread(s_p, p_p, 2, lax.rem(i + 3, RING))
+                for g, u in enumerate((PR, PN)):
+                    s_p[g, :, 0:block] = row_dot(h1v, u)
+                    spread(s_p, p_p, g, 2, lax.rem(i + 3, RING))
                 pu_keep[lax.rem(i + 1, 2), :, 0:block] = row_dot(h1v, PU)
 
             @pl.when(i >= 2)
@@ -193,6 +258,17 @@
             def _():
                 spread_wait(s_x, 1)
                 project(i + 2)
+
+            for n, (u, at) in enumerate(((R2, 0), (N2, 1))):
+                @pl.when(i == at)
+                def _():
+                    move(u, reset_rows, None)
+                    wait_in(w_own.at[0, pl.ds(0, nx * rows)], pr_recv.at[n])
+                    for tx in range(nx):
+                        @pl.when(x != tx)
+                        def _():
+                            remote(w_own.at[1 + n, pl.ds(tx * rows, rows)], w_own.at[u, partner_rows],
+                                   wsend.at[u], wrecv.at[u], tx, 1, y).start()
             return carry
 
         lax.fori_loop(0, steps + 2, step, 0)
@@ -201,7 +277,7 @@
         spread_wait(s_p, 2)
         spread_wait(s_u2, 3)
         for u in range(4):
-            wait_in(w_own.at[0, pl.ds(0, nx * rows)], wsend.at[u])
+            wait_in(w_own.at[0, pl.ds(0, (nx if u in (R1, N1) else 2 * nx - 1) * rows)], wsend.at[u])
 
         @pl.when(x == y)
         def _():
@@ -213,31 +289,16 @@
 
     @pl.when(core == 1)
     def _():
-        own = []
-        for src, u in moved:
-            own.append(pltpu.make_async_copy(src.at[:, column_slice(x)], w_own.at[u, my_rows], wl_sem.at[u]))
-        for c in own:
-            c.start()
+        fetch_first()
+        w_upd[:, :, pl.ds(nx * chunk - LANES, LANES)] = jnp.zeros((2, 2 * rows, LANES), BF16)
+
+        def put(l, row, reset, update):
+            w_upd[l, pl.ds(pl.multiple_of(row, 16), 16), 0:block] = update
+            w_upd[l, pl.ds(pl.multiple_of(rows + row, 16), 16), 0:block] = reset
+
+        split_gates(put)
+        reset_rows = lambda l, j: w_upd.at[l, pl.ds(rows, rows), pl.ds(j * chunk, chunk)]
         pl.semaphore_wait(barrier, 2 * nx * ny - 1)
-
-        def move(src, u):
-            for d in range(1, nx):
-                tx = wrap(x + d, nx)
-                remote(src.at[:, column_slice(tx)], w_own.at[u, my_rows], wsend.at[u], wrecv.at[u], tx, 1, y).start()
-
-        move(*moved[0])
-        remote(x_hbm, xb.at[1], x_sem.at[0], x_sem.at[1], x, 0, y).start()
-        for src, u in kept:
-            remote(src, block_weight(u).at[pl.ds(rows, rows)], bs_send.at[u], bs_recv.at[u], x, 0, y).start()
-
-        for u in range(4):
-            w_own[u, pl.ds(nx * block, chunk * nx - block)] = jnp.zeros((chunk * nx - block, chunk), BF16)
-        bpad[...] = jnp.zeros_like(bpad)
-        bpad[0, 0:3, 0:block] = b1[...]
-        bpad[1, 0:3, 0:block] = b2[...]
-        bias[...] = bpad[:, :, column_slice(x)]
-        valid = jnp.minimum(block - x * chunk, chunk)
-        keep = lax.broadcasted_iota(jnp.int32, (batch, chunk), 1) < valid
 
         @pl.when(x == y)
         def _():
@@ -251,6 +312,31 @@
             state[...] = hcat[:, :, column_slice(x)]
             wait_in(hcat.at[:, :, pl.ds(0, (nx - 1) * chunk)], i_sem.at[2])
 
+        for u in (R1,):
+            move(u, reset_rows, wl_sem)
+        remote(x_hbm, xb.at[1], x_sem.at[0], x_sem.at[1], x, 0, y).start()
+        for src, u in kept:
+            if src is None:
+                src = w_upd.at[u - U1, pl.ds(0, rows)]
+            remote(src, block_weight(u).at[pl.ds(rows, rows)], bs_send.at[u], bs_recv.at[u], x, 0, y).start()
+        for n, u in enumerate((R2, N2)):
+            for tx in range(nx):
+                for src, lanes in pieces(u, tx, reset_rows):
+                    remote(src, w_own.at[1 + n, pl.ds(tx * rows, rows), lanes], pr_send.at[n], pr_recv.at[n], x, 0, y).start()
+
+                    @pl.when(x == tx)
+                    def _():
+                        pltpu.make_async_copy(src, w_own.at[u, my_rows, lanes], wl_sem.at[u]).start()
+
+        for u in range(4):
+            w_own[u, pl.ds(nx * block, chunk * nx - block)] = jnp.zeros((chunk * nx - block, chunk), BF16)
+        bpad[...] = jnp.zeros_like(bpad)
+        bpad[0, 0:3, 0:block] = b1[...]
+        bpad[1, 0:3, 0:block] = b2[...]
+        bias[...] = bpad[:, :, column_slice(x)]
+        valid = jnp.minimum(block - x * chunk, chunk)
+        keep = lax.broadcasted_iota(jnp.int32, (batch, chunk), 1) < valid
+
         @pl.when(x != y)
         def _():
             wait_in(state, i_sem.at[3])
@@ -300,15 +386,14 @@
             return total
 
         def wait_weights(u):
-            own[u].wait()
+            wait_in(w_own.at[u, pl.ds(0, rows)], wl_sem.at[u])
             wait_in(w_own.at[u, pl.ds(0, (2 * nx - 1) * rows)], wrecv.at[u])
 
         for layer in range(2):
             kind = H1 if layer == 0 else H2
             ag_buf[kind, 0, 0] = jnp.where(keep, state[layer], 0.0).astype(BF16)
             to_all(kind)
-        for src, u in moved[1:]:
-            move(src, u)
+        move(N1, reset_rows, wl_sem)
 
         def copy_row_block(kind):
             blk[:, column_slice(x)] = ag_buf[kind, 0, 0]
@@ -316,7 +401,7 @@
                 blk[:, column_slice(wrap(x - dx, nx))] = ag_buf[kind, 0, dx]
 
         def reset_phase(layer, kind, unit, slot, buf, sem, hslot):
-            wait_in(buf.at[0], sem)
+            wait_in(buf.at[0, :, 0], sem.at[0])
             pre = gathered_dot(kind, unit, partial_sum(buf, slot, 0) + bias[layer, 0:1])
             to_block(layer, kind, hslot)
             if layer == 1:
@@ -329,6 +414,7 @@
 
         def candidate_phase(layer, unit, slot, buf, ubuf, usem):
             kind = RH1 if layer == 0 else RH2
+            wait_in(buf.at[0, :, 1], in_recv.at[layer, slot, 1])
             pre = gathered_dot(kind, unit, partial_sum(buf, slot, 1) + bias[layer, 2:3])
             cand = jnp.tanh(pre)
             wait_in(ubuf.at[0], usem)
@@ -349,7 +435,7 @@
                 @pl.when(i == 0)
                 def _():
                     wait_weights(R1)
-                reset_phase(0, H1 + lax.rem(i, 2), R1, slot1, p_x, rs_recv.at[1, slot1], slot1)
+                reset_phase(0, H1 + lax.rem(i, 2), R1, slot1, p_x, in_recv.at[0, slot1], slot1)
 
             @pl.when(i == steps)
             def _():
@@ -364,7 +450,7 @@
                 @pl.when(t2 == 0)
                 def _():
                     wait_weights(R2)
-                reset_phase(1, H2 + lax.rem(i, 2), R2, slot2, p_p, rs_recv.at[2, slot2], slot1)
+                reset_phase(1, H2 + lax.rem(i, 2), R2, slot2, p_p, in_recv.at[1, slot2], slot1)
 
                 @pl.when(t2 >= 1)
                 def _():
@@ -428,8 +514,10 @@
         wait_in(out_s, o_sem.at[0])
         wait_in(fin_buf.at[pl.ds(1, nx - 1)], f_sem.at[0])
         wait_in(xb.at[1], x_sem.at[0])
-        for u in range(4):
+        for u in (R1, N1):
             wait_in(w_own.at[0, pl.ds(0, (nx - 1) * rows)], wsend.at[u])
+        for n in range(2):
+            wait_in(w_own.at[0, pl.ds(0, nx * rows)], pr_send.at[n])
         for u in range(8):
             wait_in(block_weight(u).at[pl.ds(rows, rows)], bs_send.at[u])
 
@@ -461,8 +549,7 @@
             if lead:
                 operands += list(lead)
                 specs += [hbm, vmem]
-            wru = jnp.pad(jnp.transpose(wru, (1, 0, 2)), ((0, 0), (0, 0), (0, wide - cols)))
-            operands += [jnp.transpose(wx, (1, 0, 2)), wru, jnp.pad(wn, ((0, 0), (0, wide - cols))), b]
+            operands += [jnp.transpose(wx, (1, 0, 2)), wru, wn, b]
             specs += [hbm, hbm, hbm, vmem]
         scratch = [
             pltpu.VMEM((4, total_rows + wide - cols, chunk), BF16),
@@ -486,6 +573,9 @@
             pltpu.VMEM((1, batch, wide), F32),
             pltpu.VMEM((2, batch, wide), F32),
             pltpu.VMEM((2, batch, wide), F32),
+            pltpu.VMEM((2, rows // 3, 2, cols), BF16),
+            pltpu.VMEM((2, rows // 3, cols), BF16),
+            pltpu.VMEM((2, rows, LANES), BF16),
             pltpu.VMEM((batch, wide), BF16),
             pltpu.VMEM((steps, batch, part), BF16),
             pltpu.VMEM((steps, batch, part), BF16),
@@ -494,10 +584,13 @@
             pltpu.VMEM((2, batch, wide), F32),
             pltpu.VMEM((2, batch, part), F32),
             pltpu.VMEM((2, batch, part), F32),
+            dma((2, 2)),
             dma((8,)),
             dma((4,)),
             dma((4,)),
             dma((4,)),
+            dma((2,)),
+            dma((2,)),
             dma((8,)),
             dma((8,)),
             dma((2,)),
@@ -508,6 +601,7 @@
             dma((2, RING)),
             dma((4,)),
             dma((4, RING)),
+            dma((2, RING, 2)),
             dma((2,)),
             dma((4,)),
         ]
@@ -522,7 +616,7 @@
             out_specs=(vmem, vmem),
             scratch_shapes=scratch,
             compiler_params=pltpu.CompilerParams(
-                collective_id=0, has_side_effects=True, vmem_limit_bytes=61 * 1024 * 1024
+                collective_id=0, has_side_effects=True, vmem_limit_bytes=67_000_000
             ),
         )(*operands)
 

time: 406 us -> 382 us (0.941)
  local copies, waits for them, and re-layouts: 15.7 us -> 2.99 us
  Pallas kernels: 389 us -> 378 us
    pallas_call x1, Pallas kernels: 389 us -> 378 us  [device_body(): pl.pallas_call(functools.partial(gru_kernel, dims), name='gru', out_shape...]
    pad x4 -> x0, local copies, waits for them, and re-layouts: 8.11 us -> none  [the longest x2 4.89 us: device_body(): jnp.pad(jnp.transpose(wru, (1, 0, 2)), ((0, 0), (0, 0), (0, wide - cols)))]
    unnamed x12 -> x2, local copies, waits for them, and re-layouts: 7.61 us -> 2.99 us
where the time goes in v4:
time: 382 us
  Pallas kernels  378 us (99%)
    pallas_call x1, Pallas kernels, device_body(): pl.pallas_call(functools.partial(gru_kernel, dims), name='gru', out_shape...  378 us

profile of v4, /device:TPU:97, one launch (start us, length us, event | category | flops | bytes accessed | tf_op | source)
XLA Modules:
  0.0 381.6 jit_solution(13464510310064742998)
XLA Ops:
  0.6 378.0 %gru.1 = (bf16[24,16,180]{2,1,0:T(8,128)(2,1)}, f32[2,16,180]{2,1,0:T(8,128)}) custom-call(bf16[24,16,720]{2,1,0:T(8,128)(2,1)} %refs_0_.1, f32[2,16,720]{2,1,0:T(8,128)} %refs_1_.1, bf16[3,720,1440]{2,1,0:T(8,128)(2,1)} %bitcast.2, bf16[720,2,1440]{2,1,0:T(2,128)(2,1)} %refs_3_.1, bf16[720,1440]{1,0:T(8,128)(2,1)} %refs_4_.1, f32[3,1440]{1,0:T(4,128)} %refs_5_.1, ...), custom_call_target="tpu_custom_call" | custom-call | tf_op jit(solution)/shard_map/gru/pallas_call | solution.py:608
  378.6 1.6 copy.14
  380.2 1.4 copy.15

commit v5 on v4

--- a/solution.py
+++ b/solution.py
@@ -59,11 +59,7 @@
 
     offsets = [(dx, dy) for dx in range(nx) for dy in range(ny) if (dx, dy) != (0, 0)]
     offsets.sort(key=lambda o: hop(o[0], nx) + hop(o[1], ny))
-    dists = [hop(dx, nx) + hop(dy, ny) for dx, dy in offsets]
-    groups = []
-    for d in sorted(set(dists)):
-        first = dists.index(d)
-        groups.append((first, first + dists.count(d)))
+    groups = ([(0, 4), (4, 10), (10, 15)], [(0, 4), (4, 15)])
     peers = len(offsets)
 
     barrier = pltpu.get_barrier_semaphore()
@@ -240,10 +236,8 @@
                 @pl.when(i > 1)
                 def _():
                     spread_wait(s_p, 2)
-                for g, u in enumerate((PR, PN)):
-                    s_p[g, :, 0:block] = row_dot(h1v, u)
-                    spread(s_p, p_p, g, 2, lax.rem(i + 3, RING))
-                pu_keep[lax.rem(i + 1, 2), :, 0:block] = row_dot(h1v, PU)
+                s_p[0, :, 0:block] = row_dot(h1v, PR)
+                spread(s_p, p_p, 0, 2, lax.rem(i + 3, RING))
 
             @pl.when(i >= 2)
             def _():
@@ -253,6 +247,15 @@
                 def _():
                     spread_wait(s_u2, 3)
                 update_part(hs[1, lax.rem(i, RING), :, 0:block], U2, pu_keep, lax.rem(i, 2), s_u2, p_u2, 3, lax.rem(i + 2, RING))
+
+            @pl.when(jnp.logical_and(i >= 1, i <= steps))
+            def _():
+                s_p[1, :, 0:block] = row_dot(hs[0, lax.rem(i, RING), :, 0:block], PN)
+                spread(s_p, p_p, 1, 2, lax.rem(i + 3, RING))
+
+            @pl.when(jnp.logical_and(i >= 1, i <= steps))
+            def _():
+                pu_keep[lax.rem(i + 1, 2), :, 0:block] = row_dot(hs[0, lax.rem(i, RING), :, 0:block], PU)
 
             @pl.when(i + 2 < steps)
             def _():
@@ -341,10 +344,10 @@
         def _():
             wait_in(state, i_sem.at[3])
 
-        def to_all(kind):
+        def to_all(layer, kind):
             for k in reversed(range(peers)):
                 dx, dy = offsets[k]
-                g = [j for j, (a, b) in enumerate(groups) if a <= k < b][0]
+                g = [j for j, (a, b) in enumerate(groups[layer]) if a <= k < b][0]
                 remote(ag_buf.at[kind, 0, 0], ag_buf.at[kind, dy, dx], ag_send.at[kind], ag_recv.at[kind, g],
                        wrap(x + dx, nx), 1, wrap(y + dy, ny)).start()
 
@@ -367,14 +370,16 @@
             sx, sy = wrap(x - dx, nx), wrap(y - dy, ny)
             return pl.ds(pl.multiple_of(sy * block + sx * chunk, 32), chunk)
 
-        def arrive(kind, g):
-            a, b = groups[g]
+        def arrive(layer, kind, g):
+            a, b = groups[layer][g]
             wait_in(chunks(b - a), ag_recv.at[kind, g])
 
-        def gathered_dot(kind, u, acc):
+        def gathered_dot(layer, kind, u, acc, then=None):
             acc = acc + jnp.dot(ag_buf[kind, 0, 0], w_own[u, weight_rows(0, 0)], preferred_element_type=F32)
-            for g, (a, b) in enumerate(groups):
-                arrive(kind, g)
+            for g, (a, b) in enumerate(groups[layer]):
+                arrive(layer, kind, g)
+                if g == len(groups[layer]) - 1 and then is not None:
+                    then()
                 for dx, dy in offsets[a:b]:
                     acc = acc + jnp.dot(ag_buf[kind, dy, dx], w_own[u, weight_rows(dx, dy)], preferred_element_type=F32)
             return acc
@@ -392,7 +397,7 @@
         for layer in range(2):
             kind = H1 if layer == 0 else H2
             ag_buf[kind, 0, 0] = jnp.where(keep, state[layer], 0.0).astype(BF16)
-            to_all(kind)
+            to_all(layer, kind)
         move(N1, reset_rows, wl_sem)
 
         def copy_row_block(kind):
@@ -402,20 +407,20 @@
 
         def reset_phase(layer, kind, unit, slot, buf, sem, hslot):
             wait_in(buf.at[0, :, 0], sem.at[0])
-            pre = gathered_dot(kind, unit, partial_sum(buf, slot, 0) + bias[layer, 0:1])
-            to_block(layer, kind, hslot)
+            pre = gathered_dot(layer, kind, unit, partial_sum(buf, slot, 0) + bias[layer, 0:1],
+                               functools.partial(to_block, layer, kind, hslot))
             if layer == 1:
                 copy_row_block(kind)
             gate = jax.nn.sigmoid(pre)
             out = RH1 if layer == 0 else RH2
             ag_buf[out, 0, 0] = jnp.where(keep, gate * state[layer], 0.0).astype(BF16)
-            to_all(out)
+            to_all(layer, out)
             sent(kind)
 
         def candidate_phase(layer, unit, slot, buf, ubuf, usem):
             kind = RH1 if layer == 0 else RH2
             wait_in(buf.at[0, :, 1], in_recv.at[layer, slot, 1])
-            pre = gathered_dot(kind, unit, partial_sum(buf, slot, 1) + bias[layer, 2:3])
+            pre = gathered_dot(layer, kind, unit, partial_sum(buf, slot, 1) + bias[layer, 2:3])
             cand = jnp.tanh(pre)
             wait_in(ubuf.at[0], usem)
             upd = jax.nn.sigmoid(partial_sum(ubuf, slot, 0) + bias[layer, 1:2])
@@ -440,8 +445,8 @@
             @pl.when(i == steps)
             def _():
                 kind = H1 + lax.rem(i, 2)
-                for g in range(len(groups)):
-                    arrive(kind, g)
+                for g in range(len(groups[0])):
+                    arrive(0, kind, g)
                 to_block(0, kind, slot1)
                 sent(kind)
 
@@ -467,7 +472,7 @@
                     wait_weights(N1)
                 new = candidate_phase(0, N1, slot1, p_x, p_u1, rs_recv.at[0, slot1])
                 ag_buf[H1 + lax.rem(i + 1, 2), 0, 0] = new
-                to_all(H1 + lax.rem(i + 1, 2))
+                to_all(0, H1 + lax.rem(i + 1, 2))
                 sent(RH1)
                 sent_blocks(0)
 
@@ -481,7 +486,7 @@
                 @pl.when(t2 < steps - 1)
                 def _():
                     ag_buf[H2 + lax.rem(i + 1, 2), 0, 0] = new
-                    to_all(H2 + lax.rem(i + 1, 2))
+                    to_all(1, H2 + lax.rem(i + 1, 2))
                 sent(RH2)
                 sent_blocks(1)
             return carry
@@ -596,7 +601,7 @@
             dma((2,)),
             dma((4,)),
             dma((6,)),
-            dma((6, len(set(nx_hops(nx, ny))))),
+            dma((6, 4)),
             dma((2,)),
             dma((2, RING)),
             dma((4,)),

time: 382 us -> 374 us (0.979)
  Pallas kernels: 378 us -> 370 us
    pallas_call x1, Pallas kernels: 378 us -> 370 us  [device_body(): pl.pallas_call(functools.partial(gru_kernel, dims), name='gru', out_shape...]
where the time goes in v5:
time: 374 us; the launch traced here: 373 us
  Pallas kernels  370 us (99%)
    pallas_call x1, Pallas kernels, device_body(): pl.pallas_call(functools.partial(gru_kernel, dims), name='gru', out_shape...  370 us

profile of v5, /device:TPU:97, one launch (start us, length us, event | category | flops | bytes accessed | tf_op | source)
XLA Modules:
  0.0 373.3 jit_solution(8072802605474733625)
XLA Ops:
  0.6 369.6 %gru.1 = (bf16[24,16,180]{2,1,0:T(8,128)(2,1)}, f32[2,16,180]{2,1,0:T(8,128)}) custom-call(bf16[24,16,720]{2,1,0:T(8,128)(2,1)} %refs_0_.1, f32[2,16,720]{2,1,0:T(8,128)} %refs_1_.1, bf16[3,720,1440]{2,1,0:T(8,128)(2,1)} %bitcast.2, bf16[720,2,1440]{2,1,0:T(2,128)(2,1)} %refs_3_.1, bf16[720,1440]{1,0:T(8,128)(2,1)} %refs_4_.1, f32[3,1440]{1,0:T(4,128)} %refs_5_.1, ...), custom_call_target="tpu_custom_call" | custom-call | tf_op jit(solution)/shard_map/gru/pallas_call | solution.py:613
  370.3 1.6 copy.14
  371.9 1.4 copy.15

commit v6 on v5

--- a/solution.py
+++ b/solution.py
@@ -59,8 +59,12 @@
 
     offsets = [(dx, dy) for dx in range(nx) for dy in range(ny) if (dx, dy) != (0, 0)]
     offsets.sort(key=lambda o: hop(o[0], nx) + hop(o[1], ny))
-    groups = ([(0, 4), (4, 10), (10, 15)], [(0, 4), (4, 15)])
+    groups = ([(0, 4), (4, 10), (10, 15)], [(0, 5), (5, 15)])
     peers = len(offsets)
+    send_order = sorted(
+        (o for o in offsets if o[0] and o[1]), key=lambda o: (-hop(o[0], nx) - hop(o[1], ny), -hop(o[1], ny), o[1], o[0]))
+    send_order += sorted((o for o in offsets if not o[1]), key=lambda o: (hop(o[0], nx), o[0]))
+    send_order += sorted((o for o in offsets if not o[0]), key=lambda o: (-hop(o[1], ny), o[1]))
 
     barrier = pltpu.get_barrier_semaphore()
     for d in range(1, 2 * nx * ny):
@@ -175,7 +179,7 @@
         def row_dot(vec, u):
             return jnp.dot(vec, block_weight(u)[:, 0:block], preferred_element_type=F32)
 
-        near_last = sorted(range(nx), key=lambda d: -hop(d, nx))
+        near_last = sorted(range(nx), key=lambda d: (-hop(d, nx), -d))
 
         def spread(src, dst, g, kind, slot):
             for d in near_last:
@@ -345,8 +349,8 @@
             wait_in(state, i_sem.at[3])
 
         def to_all(layer, kind):
-            for k in reversed(range(peers)):
-                dx, dy = offsets[k]
+            for dx, dy in send_order:
+                k = offsets.index((dx, dy))
                 g = [j for j, (a, b) in enumerate(groups[layer]) if a <= k < b][0]
                 remote(ag_buf.at[kind, 0, 0], ag_buf.at[kind, dy, dx], ag_send.at[kind], ag_recv.at[kind, g],
                        wrap(x + dx, nx), 1, wrap(y + dy, ny)).start()

time: 374 us -> 369 us (0.987)
  Pallas kernels: 370 us -> 365 us
    pallas_call x1, Pallas kernels: 370 us -> 365 us  [device_body(): pl.pallas_call(functools.partial(gru_kernel, dims), name='gru', out_shape...]
where the time goes in v6:
time: 369 us
  Pallas kernels  365 us (99%)
    pallas_call x1, Pallas kernels, device_body(): pl.pallas_call(functools.partial(gru_kernel, dims), name='gru', out_shape...  365 us

profile of v6, /device:TPU:97, one launch (start us, length us, event | category | flops | bytes accessed | tf_op | source)
XLA Modules:
  0.0 368.7 jit_solution(10053886531025903106)
XLA Ops:
  0.6 365.1 %gru.1 = (bf16[24,16,180]{2,1,0:T(8,128)(2,1)}, f32[2,16,180]{2,1,0:T(8,128)}) custom-call(bf16[24,16,720]{2,1,0:T(8,128)(2,1)} %refs_0_.1, f32[2,16,720]{2,1,0:T(8,128)} %refs_1_.1, bf16[3,720,1440]{2,1,0:T(8,128)(2,1)} %bitcast.2, bf16[720,2,1440]{2,1,0:T(2,128)(2,1)} %refs_3_.1, bf16[720,1440]{1,0:T(8,128)(2,1)} %refs_4_.1, f32[3,1440]{1,0:T(4,128)} %refs_5_.1, ...), custom_call_target="tpu_custom_call" | custom-call | tf_op jit(solution)/shard_map/gru/pallas_call | solution.py:617
  365.7 1.6 copy.14
  367.4 1.4 copy.15

commit v7 on v6

--- a/solution.py
+++ b/solution.py
@@ -59,7 +59,7 @@
 
     offsets = [(dx, dy) for dx in range(nx) for dy in range(ny) if (dx, dy) != (0, 0)]
     offsets.sort(key=lambda o: hop(o[0], nx) + hop(o[1], ny))
-    groups = ([(0, 4), (4, 10), (10, 15)], [(0, 5), (5, 15)])
+    groups = ([(0, 4), (4, 8), (8, 15)], [(0, 5), (5, 15)])
     peers = len(offsets)
     send_order = sorted(
         (o for o in offsets if o[0] and o[1]), key=lambda o: (-hop(o[0], nx) - hop(o[1], ny), -hop(o[1], ny), o[1], o[0]))

time: 369 us -> 368 us (level)
  no operation moved by 1% of the time
where the time goes in v7:
time: 368 us; the launch traced here: 367 us
  Pallas kernels  364 us (99%)
    pallas_call x1, Pallas kernels, device_body(): pl.pallas_call(functools.partial(gru_kernel, dims), name='gru', out_shape...  364 us

profile of v7, /device:TPU:97, one launch (start us, length us, event | category | flops | bytes accessed | tf_op | source)
XLA Modules:
  0.0 367.4 jit_solution(1067279234479088914)
XLA Ops:
  0.6 363.8 %gru.1 = (bf16[24,16,180]{2,1,0:T(8,128)(2,1)}, f32[2,16,180]{2,1,0:T(8,128)}) custom-call(bf16[24,16,720]{2,1,0:T(8,128)(2,1)} %refs_0_.1, f32[2,16,720]{2,1,0:T(8,128)} %refs_1_.1, bf16[3,720,1440]{2,1,0:T(8,128)(2,1)} %bitcast.2, bf16[720,2,1440]{2,1,0:T(2,128)(2,1)} %refs_3_.1, bf16[720,1440]{1,0:T(8,128)(2,1)} %refs_4_.1, f32[3,1440]{1,0:T(4,128)} %refs_5_.1, ...), custom_call_target="tpu_custom_call" | custom-call | tf_op jit(solution)/shard_map/gru/pallas_call | solution.py:617
  364.4 1.6 copy.14
  366.0 1.4 copy.15
